TPU v7x, 128 devices: a whole 4x4x4 slice. The times are simulated.
128 devices in a mesh: seq: 16 (over x_lo, z, core), head: 4 (over y), batch: 2 (over x_hi).
Axes of the slice: x: 4 (x_hi: 2, x_lo: 2; x = x_hi * 2 + x_lo), y: 4, z: 4, core: 2. Of those that a mesh axis runs over, the one named last changes fastest.
Arguments:
- tokens: bfloat16 [32768, 2048], P(('batch', 'seq')), parts along dimension 0, may hold values from -6 to 6
- neighbor_bank: bfloat16 [512, 256, 2048], P(('batch', 'seq')), parts along dimension 0, may hold values from -2100 to 2100
- slots: int32 [512], P(('batch', 'seq')), parts along dimension 0, may hold values from 0 to 15
- w_query: bfloat16 [2048, 2048], P('seq', 'head'), may hold values from -0.125 to 0.125
- w_key: bfloat16 [2048, 2048], P('seq', 'head'), may hold values from -0.125 to 0.125
- w_value: bfloat16 [2048, 2048], P('seq', 'head'), may hold values from -0.125 to 0.125
- w_out: bfloat16 [2048, 2048], P('head', 'seq'), may hold values from -0.125 to 0.125
Outputs:
- cross_out: bfloat16 [32768, 2048], P(('batch', 'seq'), 'head'), parts along dimension 0
There are 2 independent parts, one for each index of `batch`. A program takes and returns all parts, laid end to end along the dimension named above; an argument that names none is the same for every part. Nothing has to cross between parts.
Inputs may be any that keep to these rules, and one draw needn't show every extreme that they name: Entry c picks row c // 16 * 16 + slots[c] of neighbor_bank.
All inputs are finite; a program needn't handle non-finite values.
Results may differ from a plain program's by a relative error of at most 0.006.
The roundings to bfloat16 on the way count: a program that leaves them out, or rounds other values in their place, can miss the bound.
Values may be sent and summed in bfloat16 or wider, within the bound.
No kernel may reach another device: no remote copies, remote signals or barrier semaphores. Data moves between devices by JAX's collectives and lax.ppermute only.
A program may use at most 128 MiB of HBM per device.

v0:
```python
import functools
import math

import jax
import jax.numpy as jnp
from jax import lax
from jax.experimental import pallas as pl
from jax.experimental.pallas import tpu as pltpu
from jax.sharding import PartitionSpec as P

HEAD_DIM = 128
X_LO, Z, CORE, X = 2, 4, 2, 4
CHUNK_HEADS = (2, 2)
TOKEN_PARTS = 2
GROUP = 4
LAG = 1


def route(move):
    pairs = []
    for x in range(X):
        for z in range(Z):
            for c in range(CORE):
                to_x, to_z, to_c = move(x, z, c)
                to_x, to_z, to_c = to_x % X, to_z % Z, to_c % CORE
                src = (((x % X_LO) * Z + z) * CORE + c) * 2 + x // X_LO
                dst = (((to_x % X_LO) * Z + to_z) * CORE + to_c) * 2 + to_x // X_LO
                pairs.append((src, dst))
    return pairs


Z_UP = route(lambda x, z, c: (x, z + 1, c))
Z_DOWN = route(lambda x, z, c: (x, z - 1, c))
Z_FAR = route(lambda x, z, c: (x, z + 2, c))
X_UP = route(lambda x, z, c: (x + 1, z, c))
X_DOWN = route(lambda x, z, c: (x - 1, z, c))
OTHER_CORE = route(lambda x, z, c: (x, z, c + 1))


def plane(block, pairs):
    return lax.ppermute(block, ("seq", "batch"), pairs)


def after(value, *earlier):
    return lax.optimization_barrier((value, *earlier))[0]


def gather_z(shard):
    return [shard, plane(shard, Z_UP), plane(shard, Z_DOWN), plane(shard, Z_FAR)]


def gather_x(around):
    near_pair, far_pair = jnp.stack(around[:2]), jnp.stack(around[2:])
    return [near_pair, far_pair, plane(near_pair, X_UP), plane(far_pair, X_DOWN)]


def gather_core(mine):
    return mine + [plane(p, OTHER_CORE) for p in mine]


def pack_kernel(at, heads, *refs):
    ins, (out, sem) = refs[:-2], refs[-2:]
    for i in range(3):
        for h in range(heads):
            cols = pl.ds((at + h) * HEAD_DIM, HEAD_DIM)
            pltpu.make_async_copy(ins[i].at[:, cols], out.at[i * heads + h], sem).start()
    if len(ins) > 3:
        for i in range(out.shape[0] - 3 * heads):
            rows = pl.ds(i * HEAD_DIM, HEAD_DIM)
            pltpu.make_async_copy(ins[3].at[rows], out.at[3 * heads + i], sem).start()
    pltpu.make_async_copy(out, out, sem).wait()


def pack(weights, at, heads, *tail):
    count = 3 * heads + sum(t.shape[0] // HEAD_DIM for t in tail)
    return pl.pallas_call(
        functools.partial(pack_kernel, at, heads),
        out_shape=jax.ShapeDtypeStruct((count, weights[0].shape[0], HEAD_DIM), jnp.bfloat16),
        in_specs=[pl.BlockSpec(memory_space=pl.ANY)] * (3 + len(tail)),
        out_specs=pl.BlockSpec(memory_space=pltpu.VMEM),
        scratch_shapes=[pltpu.SemaphoreType.DMA],
        name="pack",
    )(*weights, *tail)


def origins(me):
    x_lo, z, c = me // (Z * CORE), (me // CORE) % Z, me % CORE
    found = []
    for core in (c, 1 - c):
        for x in (x_lo, 1 - x_lo):
            for dz in (0, 3, 1, 2):
                found.append((x * Z + (z + dz) % Z) * CORE + core)
    return jnp.stack(found).astype(jnp.int32)


def only_head(q, h, heads):
    empty = jnp.zeros((q.shape[0], HEAD_DIM), q.dtype)
    return jnp.concatenate(
        [q[:, i * HEAD_DIM : (i + 1) * HEAD_DIM] if i == h else empty for i in range(heads)], axis=1
    )


def attend_kernel(heads, first, group, slots, rows, bank, normed, *rest):
    arrived, rest = (rest[0], rest[1:]) if first == 0 else (None, rest)
    pieces, out, ctx, w, ctx_sem, w_sem = rest[:8], *rest[8:]
    step, steps = pl.program_id(0), pl.num_programs(0)
    width = heads * HEAD_DIM
    kv_rows = bank.shape[1]
    shard = pieces[0].shape[2]

    def fetch(g, slot):
        for j in range(group):
            c = first + g * group + j
            dst = ctx.at[slot, pl.ds(j * kv_rows, kv_rows), :]
            sem = ctx_sem.at[slot]
            if first == 0 and j == 0:

                @pl.when(g == 0)
                def _():
                    pltpu.make_async_copy(arrived, dst, sem).start()

                @pl.when(g > 0)
                def _():
                    pltpu.make_async_copy(bank.at[slots[jnp.maximum(c - 1, 0)]], dst, sem).start()
            else:
                pltpu.make_async_copy(bank.at[slots[c - 1]], dst, sem).start()

    @pl.when(step == 0)
    def _():
        for i in range(8):
            for k in range(2):
                at = pl.multiple_of(rows[i * 2 + k] * shard, shard)
                pltpu.make_async_copy(
                    pieces[i].at[k, pl.ds(0, 3 * heads)], w.at[:, pl.ds(at, shard), :], w_sem
                ).start()
        fetch(0, 0)

    @pl.when(step + 1 < steps)
    def _():
        fetch(step + 1, (step + 1) % 2)

    @pl.when(step == 0)
    def _():
        pltpu.make_async_copy(w, w, w_sem).wait()

    slot = step % 2
    wq = jnp.concatenate([w[i] for i in range(heads)], axis=1)
    wkv = jnp.concatenate([w[i] for i in range(heads, 3 * heads)], axis=1)
    q = jnp.dot(normed[...], wq, preferred_element_type=jnp.float32).astype(jnp.bfloat16)
    pltpu.make_async_copy(ctx.at[slot], ctx.at[slot], ctx_sem.at[slot]).wait()
    block = normed.shape[0] // group
    kv, weights = {}, {}
    for j in range(group + 2 * LAG):
        if j < group:
            kv[j] = jnp.dot(
                ctx[slot, j * kv_rows : (j + 1) * kv_rows], wkv, preferred_element_type=jnp.float32
            ).astype(jnp.bfloat16)
        i = j - LAG
        if 0 <= i < group:
            qi = q[i * block : (i + 1) * block]
            stacked = jnp.concatenate([only_head(qi, h, heads) for h in range(heads)], axis=0)
            s = lax.dot_general(
                stacked, kv[i][:, :width], (((1,), (1,)), ((), ())), preferred_element_type=jnp.float32
            )
            s = s * (1.0 / math.sqrt(HEAD_DIM))
            e = jnp.exp(s - jnp.max(s, axis=-1, keepdims=True))
            weights[i] = (e / jnp.sum(e, axis=-1, keepdims=True)).astype(jnp.bfloat16)
        i = j - 2 * LAG
        if 0 <= i < group:
            o = jnp.dot(weights[i], kv[i][:, width:], preferred_element_type=jnp.float32).astype(jnp.bfloat16)
            for h in range(heads):
                cols = slice(h * HEAD_DIM, (h + 1) * HEAD_DIM)
                out[i * block : (i + 1) * block, cols] = o[h * block : (h + 1) * block, cols]


def attend(slots, rows, bank, arrived, normed, pieces, heads, first, blocks, group):
    model = normed.shape[1]
    kv_rows = bank.shape[1]
    arrived = [arrived] if first == 0 else []
    block = normed.shape[0] // bank.shape[0]
    width = heads * HEAD_DIM
    hbm = pl.BlockSpec(memory_space=pl.ANY)
    flops = 2 * blocks * (2 * kv_rows + block) * model * width
    return pl.pallas_call(
        functools.partial(attend_kernel, heads, first, group),
        out_shape=jax.ShapeDtypeStruct((blocks * block, width), jnp.bfloat16),
        grid_spec=pltpu.PrefetchScalarGridSpec(
            num_scalar_prefetch=2,
            grid=(blocks // group,),
            in_specs=[hbm, pl.BlockSpec((group * block, model), lambda i, *_: (first // group + i, 0))]
            + [hbm] * (len(arrived) + 8),
            out_specs=pl.BlockSpec((group * block, width), lambda i, *_: (i, 0)),
            scratch_shapes=[
                pltpu.VMEM((2, group * kv_rows, model), jnp.bfloat16),
                pltpu.VMEM((3 * heads, model, HEAD_DIM), jnp.bfloat16),
                pltpu.SemaphoreType.DMA((2,)),
                pltpu.SemaphoreType.DMA,
            ],
        ),
        cost_estimate=pl.CostEstimate(
            flops=flops, bytes_accessed=2 * blocks * kv_rows * model, transcendentals=0
        ),
        compiler_params=pltpu.CompilerParams(vmem_limit_bytes=32 * 2**20),
        name="attend",
    )(slots, rows, bank, normed, *arrived, *pieces)


def project_kernel(chunks, rows, cols, *refs):
    n = 4 * chunks
    parts, pieces = refs[:n], refs[n : n + 8]
    out, att, w, att_sem, w_sem = refs[-5:]
    deep, wide = att.shape[1] // 4, w.shape[1] // 4
    tile = pieces[0].shape[2]
    lead = pieces[0].shape[1] - deep // tile
    for i in range(8):
        for k in range(2):
            origin = rows[i * 2 + k]
            r = pl.multiple_of((origin // 4) * deep, deep)
            c = pl.multiple_of((origin % 4) * wide, wide)
            for t in range(deep // tile):
                pltpu.make_async_copy(
                    pieces[i].at[k, lead + t], w.at[pl.ds(r + t * tile, tile), pl.ds(c, wide)], w_sem
                ).start()
    at = 0
    for i in range(chunks):
        width = parts[4 * i].shape[1]
        for k in range(4):
            c = pl.multiple_of(cols[k] * deep + at, HEAD_DIM)
            pltpu.make_async_copy(parts[4 * i + k], att.at[:, pl.ds(c, width)], att_sem).start()
        at += width
    pltpu.make_async_copy(w, w, w_sem).wait()
    pltpu.make_async_copy(att, att, att_sem).wait()
    out[...] = jnp.dot(att[...], w[...], preferred_element_type=jnp.float32).astype(jnp.bfloat16)


def project(rows, cols, parts, pieces, token_part, out_rows, model, wide, before):
    tall = parts[0].shape[0]
    hbm = pl.BlockSpec(memory_space=pl.ANY)
    extra = [] if before is None else [before]
    return pl.pallas_call(
        functools.partial(project_kernel, len(parts) // 4),
        out_shape=jax.ShapeDtypeStruct((out_rows, wide), jnp.bfloat16),
        grid_spec=pltpu.PrefetchScalarGridSpec(
            num_scalar_prefetch=2,
            grid=(1,),
            in_specs=[hbm] * (len(parts) + 8 + len(extra)),
            out_specs=pl.BlockSpec((tall, wide), lambda i, *_: (token_part, 0)),
            scratch_shapes=[
                pltpu.VMEM((tall, model), jnp.bfloat16),
                pltpu.VMEM((model, wide), jnp.bfloat16),
                pltpu.SemaphoreType.DMA,
                pltpu.SemaphoreType.DMA,
            ],
        ),
        input_output_aliases={} if before is None else {2 + len(parts) + 8: 0},
        cost_estimate=pl.CostEstimate(
            flops=2 * tall * model * wide, bytes_accessed=2 * model * (tall + wide), transcendentals=0
        ),
        compiler_params=pltpu.CompilerParams(vmem_limit_bytes=16 * 2**20),
        name="project",
    )(rows, cols, *parts, *pieces, *extra)


def local(tokens, neighbor_bank, slots, w_query, w_key, w_value, w_out):
    blocks = neighbor_bank.shape[0]
    me, head_at = lax.axis_index("seq"), lax.axis_index("head")
    rows = origins(me)
    cols = jnp.stack([(head_at + d) % 4 for d in (0, 3, 1, 2)]).astype(jnp.int32)

    swap = [
        ((4 * a + j) * 4 + b, (4 * b + j) * 4 + a) for a in range(4) for b in range(4) for j in range(4)
    ]
    weights = (w_query, w_key, w_value)
    z_first = gather_z(pack(weights, 0, CHUNK_HEADS[0]))
    out_shard = lax.ppermute(w_out, ("seq", "head"), swap)
    hidden = tokens.astype(jnp.float32)
    normed = (hidden * lax.rsqrt(jnp.mean(hidden * hidden, axis=-1, keepdims=True) + 1e-06)).astype(
        jnp.bfloat16
    )
    last = lax.dynamic_index_in_dim(neighbor_bank, slots[blocks - 1], 0, keepdims=False)

    x_first = gather_x(z_first)
    second = pack(weights, CHUNK_HEADS[0], CHUNK_HEADS[1], out_shard)
    z_second = gather_z(after(second, *z_first))
    devices = lax.axis_size("seq")
    arrived = lax.ppermute(after(last, *z_first), "seq", [(i, i + 1) for i in range(devices - 1)])
    pieces = gather_core(x_first)

    part_blocks = blocks // TOKEN_PARTS
    parts = [[] for _ in range(TOKEN_PARTS)]
    ring = lambda block, d: lax.ppermute(block, "head", [(i, (i + d) % 4) for i in range(4)])
    own, n = None, 0
    for heads in CHUNK_HEADS:
        for t in reversed(range(TOKEN_PARTS)):
            x = normed if own is None else after(normed, own)
            own = attend(
                slots, rows, neighbor_bank, arrived, x, pieces, heads, t * part_blocks, part_blocks, GROUP
            )
            parts[t] += [own, ring(own, 1), ring(own, -1), ring(own, 2)]
            if n == 0:
                x_second = gather_x([after(p, own) for p in z_second])
            if n == 1:
                pieces = gather_core(x_second)
            n += 1
    out = None
    for t in reversed(range(TOKEN_PARTS)):
        out = project(
            rows, cols, parts[t], pieces, t, tokens.shape[0], tokens.shape[1], w_out.shape[0], out
        )
    return out


def solution(mesh):
    in_specs = (
        P(("batch", "seq"), None),
        P(("batch", "seq"), None, None),
        P(("batch", "seq")),
        P("seq", "head"),
        P("seq", "head"),
        P("seq", "head"),
        P("head", "seq"),
    )
    out_specs = P(("batch", "seq"), "head")

    return jax.shard_map(local, mesh=mesh, in_specs=in_specs, out_specs=out_specs, check_vma=False)
```

profile of v0, /device:TPU:8, one launch (start us, length us, event | category | flops | bytes accessed | tf_op | source)
XLA Modules:
  0.0 169.7 jit_solution(12120047913371480381)
XLA Ops:
  3.5 3.6 %collective-permute-start.2 = (bf16[6,128,128]{2,1,0:T(8,128)(2,1)}, bf16[6,128,128]{2,1,0:T(8,128)(2,1)S(1)}, u32[]{:S(2)}, u32[]{:S(2)}) collective-permute-start(bf16[6,128,128]{2,1,0:T(8,128)(2,1)} %pack.2), channel_id=1, source_target_pairs={{0,32},{8,40},{16,48},{24,56},{32,0},{40,8},{48,16},{56,24},{64,96... | collective-permute-start | bytes 589832 | tf_op jit(solution)/shard_map/ppermute | solution.py:41
  8.1 2.3 %collective-permute-start.13 = (bf16[512,128]{1,0:T(8,128)(2,1)}, bf16[512,128]{1,0:T(8,128)(2,1)S(1)}, u32[]{:S(2)}, u32[]{:S(2)}) collective-permute-start(bf16[512,128]{1,0:T(8,128)(2,1)} %param.13), channel_id=1, source_target_pairs={{0,0},{8,8},{16,16},{24,24},{2,32},{10,40},{18,48},{26,56},{4,64},... | collective-permute-start | bytes 393224 | tf_op jit(solution)/shard_map/ppermute | solution.py:275
  11.8 2.4 %collective-permute-start.3 = (bf16[2,6,128,128]{3,2,1,0:T(8,128)(2,1)S(1)}, bf16[2,6,128,128]{3,2,1,0:T(8,128)(2,1)S(1)}, u32[]{:S(2)}, u32[]{:S(2)}) collective-permute-start(bf16[2,6,128,128]{3,2,1,0:T(8,128)(2,1)S(1)} %pad_maximum_fusion.2.rest_0_.rest_1_), channel_id=1, source_target_pairs={{0,64},{8,72},{16,80},{24,88},{32,96},{40,104},{48,112},{56,120},{... | collective-permute-start | bytes 1179656 | tf_op jit(solution)/shard_map/ppermute | solution.py:41
  14.1 4.9 %collective-permute-done.2 = bf16[6,128,128]{2,1,0:T(8,128)(2,1)S(1)} collective-permute-done((bf16[6,128,128]{2,1,0:T(8,128)(2,1)}, bf16[6,128,128]{2,1,0:T(8,128)(2,1)S(1)}, u32[]{:S(2)}, u32[]{:S(2)}) %collective-permute-start.2) | collective-permute-done | bytes 196640 | tf_op jit(solution)/shard_map/ppermute | solution.py:41
  20.3 3.1 %fusion = f32[1024]{0:T(1024)S(1)} fusion(bf16[1024,2048]{1,0:T(8,128)(2,1)} %param.7), kind=kLoop, calls=%fused_computation.2 | loop fusion | flops 6290432 | bytes 4198400 | tf_op jit(solution)/shard_map/reduce_sum | solution.py:277
  24.0 5.1 %collective-permute-done.4.rest_3_.rest_4_ = bf16[2,6,128,128]{3,2,1,0:T(8,128)(2,1)S(1)} collective-permute-done((bf16[2,6,128,128]{3,2,1,0:T(8,128)(2,1)S(1)}, bf16[2,6,128,128]{3,2,1,0:T(8,128)(2,1)S(1)}, u32[]{:S(2)}, u32[]{:S(2)}) %collective-permute-start.4) | collective-permute-done | bytes 393248 | tf_op jit(solution)/shard_map/ppermute | solution.py:41
  29.1 2.7 %fusion.1.normed = bf16[1024,2048]{1,0:T(8,128)(2,1)} fusion(bf16[1024,2048]{1,0:T(8,128)(2,1)S(1)} %copy-done.41, f32[1024]{0:T(1024)S(1)} %add_rsqrt_fusion), kind=kLoop, calls=%fused_computation.3 | loop fusion | flops 6291456 | bytes 8392704 | tf_op jit(solution)/shard_map/convert_element_type | solution.py:277
  34.6 2.3 %dynamic-slice_bitcast_fusion = bf16[256,2048]{1,0:T(8,128)(2,1)} fusion(bf16[16,256,2048]{2,1,0:T(8,128)(2,1)} %bank.7, s32[]{:T(128)S(6)} %select_n.90), kind=kLoop, calls=%fused_computation.4 | loop fusion | bytes 2097156 | tf_op jit(solution)/shard_map/jit(dynamic_index_in_dim)/squeeze | solution.py:280
  41.5 2.6 %collective-permute-start.15 = (bf16[10,128,128]{2,1,0:T(8,128)(2,1)}, bf16[10,128,128]{2,1,0:T(8,128)(2,1)S(1)}, u32[]{:S(2)}, u32[]{:S(2)}) collective-permute-start(bf16[10,128,128]{2,1,0:T(8,128)(2,1)} %pack.3), channel_id=1, source_target_pairs={{0,48},{8,56},{16,0},{24,8},{32,16},{40,24},{48,32},{56,40},{64,11... | collective-permute-start | bytes 983048 | tf_op jit(solution)/shard_map/ppermute | solution.py:41
  46.0 2.2 %copy-done = bf16[1024,2048]{1,0:T(8,128)(2,1)S(1)} copy-done((bf16[1024,2048]{1,0:T(8,128)(2,1)S(1)}, bf16[1024,2048]{1,0:T(8,128)(2,1)}, u32[]{:S(2)}) %copy-start) | copy-done | bytes 4194328
  48.2 11.1 %attend.4.refs_0_ = bf16[512,256]{1,0:T(8,128)(2,1)S(1)} custom-call(s32[16]{0:T(128)S(1)} %copy-done.40, s32[16]{0:T(128)S(1)} %stack.118.rows, bf16[16,256,2048]{2,1,0:T(8,128)(2,1)} %bank.7, bf16[1024,2048]{1,0:T(8,128)(2,1)S(1)} %copy-done, bf16[2,6,128,128]{3,2,1,0:T(8,128)(2,1)S(1)} %pad_maximum_fusion.2.rest_0_.rest_1_, ...), custom_call_target="tpu_custom_call" | custom-call | flops 4831838208 | bytes 8388608 | tf_op jit(solution)/shard_map/attend/pallas_call | solution.py:184
  59.4 11.1 %collective-permute-start.17 = (bf16[2,10,128,128]{3,2,1,0:T(8,128)(2,1)S(1)}, bf16[2,10,128,128]{3,2,1,0:T(8,128)(2,1)S(1)}, u32[]{:S(2)}, u32[]{:S(2)}) collective-permute-start(bf16[2,10,128,128]{3,2,1,0:T(8,128)(2,1)S(1)} %pad_maximum_fusion.rest_0_.rest_1_.refs_8_), channel_id=1, source_target_pairs={{0,64},{8,72},{16,80},{24,88},{32,96},{40,104},{48,112},{56,120},{... | collective-permute-start | bytes 1966088 | tf_op jit(solution)/shard_map/ppermute | solution.py:41
  71.3 13.1 %collective-permute-done.17.rest_2_.rest_3_.refs_10_ = bf16[2,10,128,128]{3,2,1,0:T(8,128)(2,1)S(1)} collective-permute-done((bf16[2,10,128,128]{3,2,1,0:T(8,128)(2,1)S(1)}, bf16[2,10,128,128]{3,2,1,0:T(8,128)(2,1)S(1)}, u32[]{:S(2)}, u32[]{:S(2)}) %collective-permute-start.17) | collective-permute-done | bytes 655392 | tf_op jit(solution)/shard_map/ppermute | solution.py:41
  84.3 2.3 %collective-permute-done.18.rest_3_.rest_4_.refs_11_ = bf16[2,10,128,128]{3,2,1,0:T(8,128)(2,1)S(1)} collective-permute-done((bf16[2,10,128,128]{3,2,1,0:T(8,128)(2,1)S(1)}, bf16[2,10,128,128]{3,2,1,0:T(8,128)(2,1)S(1)}, u32[]{:S(2)}, u32[]{:S(2)}) %collective-permute-start.18) | collective-permute-done | bytes 655392 | tf_op jit(solution)/shard_map/ppermute | solution.py:41
  94.7 10.5 %attend.5.refs_0_ = bf16[512,256]{1,0:T(8,128)(2,1)} custom-call(s32[16]{0:T(128)S(1)} %copy-done.40, s32[16]{0:T(128)S(1)} %stack.118.rows, bf16[16,256,2048]{2,1,0:T(8,128)(2,1)} %bank.7, bf16[1024,2048]{1,0:T(8,128)(2,1)S(1)} %copy-done, bf16[256,2048]{1,0:T(8,128)(2,1)S(1)} %collective-permute-done.9.rest_0_, bf16[2,6,128,128]{3,2,1,0:T(8,128)(2,1)S(1)} %copy-done.9, ...), custom_call_target="tpu_custom_call" | custom-call | flops 4831838208 | bytes 8388608 | tf_op jit(solution)/shard_map/attend/pallas_call | solution.py:184
  105.2 2.1 %collective-permute-start.27 = (bf16[512,256]{1,0:T(8,128)(2,1)S(1)}, bf16[512,256]{1,0:T(8,128)(2,1)S(1)}, u32[]{:S(2)}, u32[]{:S(2)}) collective-permute-start(bf16[512,256]{1,0:T(8,128)(2,1)S(1)} %attend.4.refs_0_), channel_id=1, source_target_pairs={{0,6},{2,0},{4,2},{6,4},{1,7},{3,1},{5,3},{7,5},{8,14},{10,8},{12,... | collective-permute-start | bytes 786440 | tf_op jit(solution)/shard_map/ppermute | solution.py:291
  107.3 3.9 %collective-permute-start.28 = (bf16[512,256]{1,0:T(8,128)(2,1)S(1)}, bf16[512,256]{1,0:T(8,128)(2,1)S(1)}, u32[]{:S(2)}, u32[]{:S(2)}) collective-permute-start(bf16[512,256]{1,0:T(8,128)(2,1)S(1)} %attend.4.refs_0_), channel_id=1, source_target_pairs={{0,4},{2,6},{4,0},{6,2},{1,5},{3,7},{5,1},{7,3},{8,12},{10,14},{12... | collective-permute-start | bytes 786440 | tf_op jit(solution)/shard_map/ppermute | solution.py:291
  111.9 11.1 %attend.6.refs_4_ = bf16[512,256]{1,0:T(8,128)(2,1)S(1)} custom-call(s32[16]{0:T(128)S(1)} %copy-done.40, s32[16]{0:T(128)S(1)} %stack.118.rows, bf16[16,256,2048]{2,1,0:T(8,128)(2,1)} %bank.7, bf16[1024,2048]{1,0:T(8,128)(2,1)S(1)} %copy-done, bf16[2,10,128,128]{3,2,1,0:T(8,128)(2,1)S(1)} %pad_maximum_fusion.rest_0_.rest_1_.refs_8_, ...), custom_call_target="tpu_custom_call" | custom-call | flops 4831838208 | bytes 8388608 | tf_op jit(solution)/shard_map/attend/pallas_call | solution.py:184
  125.1 2.2 %collective-permute-start.31 = (bf16[512,256]{1,0:T(8,128)(2,1)S(1)}, bf16[512,256]{1,0:T(8,128)(2,1)S(1)}, u32[]{:S(2)}, u32[]{:S(2)}) collective-permute-start(bf16[512,256]{1,0:T(8,128)(2,1)S(1)} %attend.6.refs_4_), channel_id=1, source_target_pairs={{0,4},{2,6},{4,0},{6,2},{1,5},{3,7},{5,1},{7,3},{8,12},{10,14},{12... | collective-permute-start | bytes 786440 | tf_op jit(solution)/shard_map/ppermute | solution.py:291
  127.2 10.6 %attend.7.refs_4_ = bf16[512,256]{1,0:T(8,128)(2,1)} custom-call(s32[16]{0:T(128)S(1)} %copy-done.40, s32[16]{0:T(128)S(1)} %stack.118.rows, bf16[16,256,2048]{2,1,0:T(8,128)(2,1)} %bank.7, bf16[1024,2048]{1,0:T(8,128)(2,1)S(1)} %copy-done, bf16[256,2048]{1,0:T(8,128)(2,1)S(1)} %collective-permute-done.9.rest_0_, ...), custom_call_target="tpu_custom_call" | custom-call | flops 4831838208 | bytes 8388608 | tf_op jit(solution)/shard_map/attend/pallas_call | solution.py:184
  139.9 2.7 %collective-permute-start.12 = (bf16[512,256]{1,0:T(8,128)(2,1)}, bf16[512,256]{1,0:T(8,128)(2,1)}, u32[]{:S(2)}, u32[]{:S(2)}) collective-permute-start(bf16[512,256]{1,0:T(8,128)(2,1)} %attend.5.refs_0_), channel_id=1, source_target_pairs={{0,4},{2,6},{4,0},{6,2},{1,5},{3,7},{5,1},{7,3},{8,12},{10,14},{12... | collective-permute-start | bytes 786440 | tf_op jit(solution)/shard_map/ppermute | solution.py:291
  157.6 3.5 %project.2.refs_16_ = bf16[1024,512]{1,0:T(8,128)(2,1)} custom-call(s32[16]{0:T(128)S(1)} %stack.118.rows, s32[4]{0:T(128)S(1)} %pad_add_fusion.cols, bf16[512,256]{1,0:T(8,128)(2,1)S(1)} %attend.4.refs_0_, bf16[512,256]{1,0:T(8,128)(2,1)S(1)} %copy-done.29, bf16[512,256]{1,0:T(8,128)(2,1)S(1)} %copy-done.31, bf16[512,256]{1,0:T(8,128)(2,1)S(1)} %copy-done.33, ...), custom_call_target="tpu_custom_call" | custom-call | flops 1073741824 | bytes 4194304 | tf_op jit(solution)/shard_map/project/pallas_call | solution.py:240
  161.2 3.7 %collective-permute-done.25.refs_7_ = bf16[512,256]{1,0:T(8,128)(2,1)} collective-permute-done((bf16[512,256]{1,0:T(8,128)(2,1)}, bf16[512,256]{1,0:T(8,128)(2,1)}, u32[]{:S(2)}, u32[]{:S(2)}) %collective-permute-start.25) | collective-permute-done | bytes 262176 | tf_op jit(solution)/shard_map/ppermute | solution.py:291
  164.9 4.7 %project.3 = bf16[1024,512]{1,0:T(8,128)(2,1)} custom-call(s32[16]{0:T(128)S(1)} %stack.118.rows, s32[4]{0:T(128)S(1)} %pad_add_fusion.cols, bf16[512,256]{1,0:T(8,128)(2,1)} %attend.5.refs_0_, bf16[512,256]{1,0:T(8,128)(2,1)S(1)} %copy-done.27, bf16[512,256]{1,0:T(8,128)(2,1)} %collective-permute-done.11.refs_2_, ...), custom_call_target="tpu_custom_call", output_to_operand_aliasing={{}: (18, {})} | custom-call | flops 1073741824 | bytes 4194304 | tf_op jit(solution)/shard_map/project/pallas_call | solution.py:240
  (147 shorter events, 43.6 us)
Async XLA Ops:
  8.1 28.8 %collective-permute-start.13 = (bf16[512,128]{1,0:T(8,128)(2,1)}, bf16[512,128]{1,0:T(8,128)(2,1)S(1)}, u32[]{:S(2)}, u32[]{:S(2)}) collective-permute-start(bf16[512,128]{1,0:T(8,128)(2,1)} %param.13), channel_id=1, source_target_pairs={{0,0},{8,8},{16,16},{24,24},{2,32},{10,40},{18,48},{26,56},{4,64},... | collective-permute-start | bytes 393224 | tf_op jit(solution)/shard_map/ppermute | solution.py:275
  23.3 17.9 %collective-permute-start.5 = (bf16[2,6,128,128]{3,2,1,0:T(8,128)(2,1)S(1)}, bf16[2,6,128,128]{3,2,1,0:T(8,128)(2,1)S(1)}, u32[]{:S(2)}, u32[]{:S(2)}) collective-permute-start(bf16[2,6,128,128]{3,2,1,0:T(8,128)(2,1)S(1)} %pad_maximum_fusion.2.rest_0_.rest_1_), channel_id=1, source_target_pairs={{0,8},{8,0},{16,24},{24,16},{32,40},{40,32},{48,56},{56,48},{64,72... | collective-permute-start | bytes 1179656 | tf_op jit(solution)/shard_map/ppermute | solution.py:41
  23.4 18.0 %collective-permute-start.6 = (bf16[2,6,128,128]{3,2,1,0:T(8,128)(2,1)S(1)}, bf16[2,6,128,128]{3,2,1,0:T(8,128)(2,1)S(1)}, u32[]{:S(2)}, u32[]{:S(2)}) collective-permute-start(bf16[2,6,128,128]{3,2,1,0:T(8,128)(2,1)S(1)} %pad_maximum_fusion.3.rest_1_.rest_2_), channel_id=1, source_target_pairs={{0,8},{8,0},{16,24},{24,16},{32,40},{40,32},{48,56},{56,48},{64,72... | collective-permute-start | bytes 1179656 | tf_op jit(solution)/shard_map/ppermute | solution.py:41
  24.0 20.1 %collective-permute-start.7 = (bf16[2,6,128,128]{3,2,1,0:T(8,128)(2,1)S(1)}, bf16[2,6,128,128]{3,2,1,0:T(8,128)(2,1)S(1)}, u32[]{:S(2)}, u32[]{:S(2)}) collective-permute-start(bf16[2,6,128,128]{3,2,1,0:T(8,128)(2,1)S(1)} %collective-permute-done.3.rest_2_.rest_3_), channel_id=1, source_target_pairs={{0,8},{8,0},{16,24},{24,16},{32,40},{40,32},{48,56},{56,48},{64,72... | collective-permute-start | bytes 1179656 | tf_op jit(solution)/shard_map/ppermute | solution.py:41
  39.3 20.0 %collective-permute-start.14 = (bf16[10,128,128]{2,1,0:T(8,128)(2,1)}, bf16[10,128,128]{2,1,0:T(8,128)(2,1)S(1)}, u32[]{:S(2)}, u32[]{:S(2)}) collective-permute-start(bf16[10,128,128]{2,1,0:T(8,128)(2,1)} %pack.3), channel_id=1, source_target_pairs={{0,16},{8,24},{16,32},{24,40},{32,48},{40,56},{48,0},{56,8},{64,80... | collective-permute-start | bytes 983048 | tf_op jit(solution)/shard_map/ppermute | solution.py:41
  41.3 18.1 %collective-permute-start.16 = (bf16[10,128,128]{2,1,0:T(8,128)(2,1)}, bf16[10,128,128]{2,1,0:T(8,128)(2,1)S(1)}, u32[]{:S(2)}, u32[]{:S(2)}) collective-permute-start(bf16[10,128,128]{2,1,0:T(8,128)(2,1)} %pack.3), channel_id=1, source_target_pairs={{0,32},{8,40},{16,48},{24,56},{32,0},{40,8},{48,16},{56,24},{64,96... | collective-permute-start | bytes 983048 | tf_op jit(solution)/shard_map/ppermute | solution.py:41
  41.5 17.9 %collective-permute-start.15 = (bf16[10,128,128]{2,1,0:T(8,128)(2,1)}, bf16[10,128,128]{2,1,0:T(8,128)(2,1)S(1)}, u32[]{:S(2)}, u32[]{:S(2)}) collective-permute-start(bf16[10,128,128]{2,1,0:T(8,128)(2,1)} %pack.3), channel_id=1, source_target_pairs={{0,48},{8,56},{16,0},{24,8},{32,16},{40,24},{48,32},{56,40},{64,11... | collective-permute-start | bytes 983048 | tf_op jit(solution)/shard_map/ppermute | solution.py:41
  44.0 42.6 %collective-permute-start.9 = (bf16[256,2048]{1,0:T(8,128)(2,1)}, bf16[256,2048]{1,0:T(8,128)(2,1)S(1)}, u32[]{:S(2)}, u32[]{:S(2)}) collective-permute-start(bf16[256,2048]{1,0:T(8,128)(2,1)} %dynamic-slice_bitcast_fusion), channel_id=1, source_target_pairs={{0,8},{8,16},{16,24},{24,32},{32,40},{40,48},{48,56},{56,64},{64,7... | collective-permute-start | bytes 3145736 | tf_op jit(solution)/shard_map/ppermute | solution.py:286
  59.4 24.9 %collective-permute-start.17 = (bf16[2,10,128,128]{3,2,1,0:T(8,128)(2,1)S(1)}, bf16[2,10,128,128]{3,2,1,0:T(8,128)(2,1)S(1)}, u32[]{:S(2)}, u32[]{:S(2)}) collective-permute-start(bf16[2,10,128,128]{3,2,1,0:T(8,128)(2,1)S(1)} %pad_maximum_fusion.rest_0_.rest_1_.refs_8_), channel_id=1, source_target_pairs={{0,64},{8,72},{16,80},{24,88},{32,96},{40,104},{48,112},{56,120},{... | collective-permute-start | bytes 1966088 | tf_op jit(solution)/shard_map/ppermute | solution.py:41
  70.7 34.5 %collective-permute-start.19 = (bf16[2,10,128,128]{3,2,1,0:T(8,128)(2,1)S(1)}, bf16[2,10,128,128]{3,2,1,0:T(8,128)(2,1)S(1)}, u32[]{:S(2)}, u32[]{:S(2)}) collective-permute-start(bf16[2,10,128,128]{3,2,1,0:T(8,128)(2,1)S(1)} %pad_maximum_fusion.rest_0_.rest_1_.refs_8_), channel_id=1, source_target_pairs={{0,8},{8,0},{16,24},{24,16},{32,40},{40,32},{48,56},{56,48},{64,72... | collective-permute-start | bytes 1966088 | tf_op jit(solution)/shard_map/ppermute | solution.py:41
  70.8 36.5 %collective-permute-start.20 = (bf16[2,10,128,128]{3,2,1,0:T(8,128)(2,1)S(1)}, bf16[2,10,128,128]{3,2,1,0:T(8,128)(2,1)S(1)}, u32[]{:S(2)}, u32[]{:S(2)}) collective-permute-start(bf16[2,10,128,128]{3,2,1,0:T(8,128)(2,1)S(1)} %pad_maximum_fusion.1.rest_1_.rest_2_.refs_9_), channel_id=1, source_target_pairs={{0,8},{8,0},{16,24},{24,16},{32,40},{40,32},{48,56},{56,48},{64,72... | collective-permute-start | bytes 1966088 | tf_op jit(solution)/shard_map/ppermute | solution.py:41
  84.3 26.9 %collective-permute-start.21 = (bf16[2,10,128,128]{3,2,1,0:T(8,128)(2,1)S(1)}, bf16[2,10,128,128]{3,2,1,0:T(8,128)(2,1)S(1)}, u32[]{:S(2)}, u32[]{:S(2)}) collective-permute-start(bf16[2,10,128,128]{3,2,1,0:T(8,128)(2,1)S(1)} %collective-permute-done.17.rest_2_.rest_3_.refs_10_), channel_id=1, source_target_pairs={{0,8},{8,0},{16,24},{24,16},{32,40},{40,32},{48,56},{56,48},{64,72... | collective-permute-start | bytes 1966088 | tf_op jit(solution)/shard_map/ppermute | solution.py:41
  86.7 25.2 %collective-permute-start.22 = (bf16[2,10,128,128]{3,2,1,0:T(8,128)(2,1)S(1)}, bf16[2,10,128,128]{3,2,1,0:T(8,128)(2,1)S(1)}, u32[]{:S(2)}, u32[]{:S(2)}) collective-permute-start(bf16[2,10,128,128]{3,2,1,0:T(8,128)(2,1)S(1)} %collective-permute-done.18.rest_3_.rest_4_.refs_11_), channel_id=1, source_target_pairs={{0,8},{8,0},{16,24},{24,16},{32,40},{40,32},{48,56},{56,48},{64,72... | collective-permute-start | bytes 1966088 | tf_op jit(solution)/shard_map/ppermute | solution.py:41
  86.7 36.4 %collective-permute-start.26 = (bf16[512,256]{1,0:T(8,128)(2,1)S(1)}, bf16[512,256]{1,0:T(8,128)(2,1)S(1)}, u32[]{:S(2)}, u32[]{:S(2)}) collective-permute-start(bf16[512,256]{1,0:T(8,128)(2,1)S(1)} %attend.4.refs_0_), channel_id=1, source_target_pairs={{0,2},{2,4},{4,6},{6,0},{1,3},{3,5},{5,7},{7,1},{8,10},{10,12},{12... | collective-permute-start | bytes 786440 | tf_op jit(solution)/shard_map/ppermute | solution.py:291
  105.2 19.8 %collective-permute-start.27 = (bf16[512,256]{1,0:T(8,128)(2,1)S(1)}, bf16[512,256]{1,0:T(8,128)(2,1)S(1)}, u32[]{:S(2)}, u32[]{:S(2)}) collective-permute-start(bf16[512,256]{1,0:T(8,128)(2,1)S(1)} %attend.4.refs_0_), channel_id=1, source_target_pairs={{0,6},{2,0},{4,2},{6,4},{1,7},{3,1},{5,3},{7,5},{8,14},{10,8},{12,... | collective-permute-start | bytes 786440 | tf_op jit(solution)/shard_map/ppermute | solution.py:291
  107.3 30.5 %collective-permute-start.28 = (bf16[512,256]{1,0:T(8,128)(2,1)S(1)}, bf16[512,256]{1,0:T(8,128)(2,1)S(1)}, u32[]{:S(2)}, u32[]{:S(2)}) collective-permute-start(bf16[512,256]{1,0:T(8,128)(2,1)S(1)} %attend.4.refs_0_), channel_id=1, source_target_pairs={{0,4},{2,6},{4,0},{6,2},{1,5},{3,7},{5,1},{7,3},{8,12},{10,14},{12... | collective-permute-start | bytes 786440 | tf_op jit(solution)/shard_map/ppermute | solution.py:291
  111.2 28.0 %collective-permute-start.10 = (bf16[512,256]{1,0:T(8,128)(2,1)}, bf16[512,256]{1,0:T(8,128)(2,1)S(1)}, u32[]{:S(2)}, u32[]{:S(2)}) collective-permute-start(bf16[512,256]{1,0:T(8,128)(2,1)} %attend.5.refs_0_), channel_id=1, source_target_pairs={{0,2},{2,4},{4,6},{6,0},{1,3},{3,5},{5,7},{7,1},{8,10},{10,12},{12... | collective-permute-start | bytes 786440 | tf_op jit(solution)/shard_map/ppermute | solution.py:291
  122.9 19.7 %collective-permute-start.29 = (bf16[512,256]{1,0:T(8,128)(2,1)S(1)}, bf16[512,256]{1,0:T(8,128)(2,1)S(1)}, u32[]{:S(2)}, u32[]{:S(2)}) collective-permute-start(bf16[512,256]{1,0:T(8,128)(2,1)S(1)} %attend.6.refs_4_), channel_id=1, source_target_pairs={{0,2},{2,4},{4,6},{6,0},{1,3},{3,5},{5,7},{7,1},{8,10},{10,12},{12... | collective-permute-start | bytes 786440 | tf_op jit(solution)/shard_map/ppermute | solution.py:291
  123.1 20.9 %collective-permute-start.30 = (bf16[512,256]{1,0:T(8,128)(2,1)S(1)}, bf16[512,256]{1,0:T(8,128)(2,1)S(1)}, u32[]{:S(2)}, u32[]{:S(2)}) collective-permute-start(bf16[512,256]{1,0:T(8,128)(2,1)S(1)} %attend.6.refs_4_), channel_id=1, source_target_pairs={{0,6},{2,0},{4,2},{6,4},{1,7},{3,1},{5,3},{7,5},{8,14},{10,8},{12,... | collective-permute-start | bytes 786440 | tf_op jit(solution)/shard_map/ppermute | solution.py:291
  125.1 21.0 %collective-permute-start.31 = (bf16[512,256]{1,0:T(8,128)(2,1)S(1)}, bf16[512,256]{1,0:T(8,128)(2,1)S(1)}, u32[]{:S(2)}, u32[]{:S(2)}) collective-permute-start(bf16[512,256]{1,0:T(8,128)(2,1)S(1)} %attend.6.refs_4_), channel_id=1, source_target_pairs={{0,4},{2,6},{4,0},{6,2},{1,5},{3,7},{5,1},{7,3},{8,12},{10,14},{12... | collective-permute-start | bytes 786440 | tf_op jit(solution)/shard_map/ppermute | solution.py:291
  138.6 22.6 %collective-permute-start.11 = (bf16[512,256]{1,0:T(8,128)(2,1)}, bf16[512,256]{1,0:T(8,128)(2,1)}, u32[]{:S(2)}, u32[]{:S(2)}) collective-permute-start(bf16[512,256]{1,0:T(8,128)(2,1)} %attend.5.refs_0_), channel_id=1, source_target_pairs={{0,6},{2,0},{4,2},{6,4},{1,7},{3,1},{5,3},{7,5},{8,14},{10,8},{12,... | collective-permute-start | bytes 786440 | tf_op jit(solution)/shard_map/ppermute | solution.py:291
  139.9 21.2 %collective-permute-start.12 = (bf16[512,256]{1,0:T(8,128)(2,1)}, bf16[512,256]{1,0:T(8,128)(2,1)}, u32[]{:S(2)}, u32[]{:S(2)}) collective-permute-start(bf16[512,256]{1,0:T(8,128)(2,1)} %attend.5.refs_0_), channel_id=1, source_target_pairs={{0,4},{2,6},{4,0},{6,2},{1,5},{3,7},{5,1},{7,3},{8,12},{10,14},{12... | collective-permute-start | bytes 786440 | tf_op jit(solution)/shard_map/ppermute | solution.py:291
  143.3 17.8 %collective-permute-start.23 = (bf16[512,256]{1,0:T(8,128)(2,1)}, bf16[512,256]{1,0:T(8,128)(2,1)}, u32[]{:S(2)}, u32[]{:S(2)}) collective-permute-start(bf16[512,256]{1,0:T(8,128)(2,1)} %attend.7.refs_4_), channel_id=1, source_target_pairs={{0,2},{2,4},{4,6},{6,0},{1,3},{3,5},{5,7},{7,1},{8,10},{10,12},{12... | collective-permute-start | bytes 786440 | tf_op jit(solution)/shard_map/ppermute | solution.py:291
  146.8 18.1 %collective-permute-start.25 = (bf16[512,256]{1,0:T(8,128)(2,1)}, bf16[512,256]{1,0:T(8,128)(2,1)}, u32[]{:S(2)}, u32[]{:S(2)}) collective-permute-start(bf16[512,256]{1,0:T(8,128)(2,1)} %attend.7.refs_4_), channel_id=1, source_target_pairs={{0,4},{2,6},{4,0},{6,2},{1,5},{3,7},{5,1},{7,3},{8,12},{10,14},{12... | collective-permute-start | bytes 786440 | tf_op jit(solution)/shard_map/ppermute | solution.py:291
  (52 other events, 526.6 us)
where the time goes:
time: 171 us; the launch traced here: 170 us
  Pallas kernels  54.6 us (32%)
  starting transfers between devices  48.8 us (29%)
  waiting for transfers between devices  29.4 us (17%)
  local copies, waits for them, and re-layouts  27.3 us (16%)
  other arithmetic  7.01 us (4%)
  between operations  2.63 us (2%)
    pallas_call x4, Pallas kernels, attend(): pl.pallas_call(functools.partial(attend_kernel, heads, first, group), out...  43.2 us
    ppermute x18, starting transfers between devices, plane(): return lax.ppermute(block, ('seq', 'batch'), pairs)  27.4 us
    ppermute x18, waiting for transfers between devices, plane(): return lax.ppermute(block, ('seq', 'batch'), pairs)  25.7 us
    unnamed x88, local copies, waits for them, and re-layouts  24.3 us
    ppermute x12, starting transfers between devices, local(): lax.ppermute(block, 'head', [(i, (i + d) % 4) for i in range(4)])  17.2 us
    pallas_call x2, Pallas kernels, project(): pl.pallas_call(functools.partial(project_kernel, len(parts) // 4), out_sh...  8.18 us
    ppermute x12, waiting for transfers between devices, local(): lax.ppermute(block, 'head', [(i, (i + d) % 4) for i in range(4)])  3.73 us
  transfers between devices with their start and end apart: 32, of which 6 were waited for; matrix products, arithmetic and copies ran while one was open for 6% of the time, Pallas kernels for 29%

commit v1 on v0

v1 whole, which is shorter than its diff:
```python
import functools
import math

import jax
import jax.numpy as jnp
from jax import lax
from jax.experimental import pallas as pl
from jax.experimental.pallas import tpu as pltpu
from jax.sharding import PartitionSpec as P

HEAD_DIM = 128
X_LO, Z, CORE, X = 2, 4, 2, 4
CHUNK_HEADS = (2, 2)
RUNS = ((12, 4), (0, 12))
GROUP = 4
LAG = 1
AHEAD = 1


def route(move):
    pairs = []
    for x in range(X):
        for z in range(Z):
            for c in range(CORE):
                to_x, to_z, to_c = move(x, z, c)
                to_x, to_z, to_c = to_x % X, to_z % Z, to_c % CORE
                src = (((x % X_LO) * Z + z) * CORE + c) * 2 + x // X_LO
                dst = (((to_x % X_LO) * Z + to_z) * CORE + to_c) * 2 + to_x // X_LO
                pairs.append((src, dst))
    return pairs


Z_UP = route(lambda x, z, c: (x, z + 1, c))
Z_DOWN = route(lambda x, z, c: (x, z - 1, c))
Z_FAR = route(lambda x, z, c: (x, z + 2, c))
X_UP = route(lambda x, z, c: (x + 1, z, c))
X_DOWN = route(lambda x, z, c: (x - 1, z, c))
OTHER_CORE = route(lambda x, z, c: (x, z, c + 1))


def plane(block, pairs):
    return lax.ppermute(block, ("seq", "batch"), pairs)


def after(value, *earlier):
    return lax.optimization_barrier((value, *earlier))[0]


def gather_z(shard):
    return [shard, plane(shard, Z_UP), plane(shard, Z_DOWN), plane(shard, Z_FAR)]


def gather_x(around):
    near_pair, far_pair = jnp.stack(around[:2]), jnp.stack(around[2:])
    return [near_pair, far_pair, plane(near_pair, X_UP), plane(far_pair, X_DOWN)]


def gather_core(mine):
    near = [plane(p, OTHER_CORE) for p in mine[:2]]
    far = [plane(p, OTHER_CORE) for p in mine[2:]]
    return mine + near + far


def prepare_kernel(slots, bank, tokens, normed, last, sem):
    step = pl.program_id(0)

    @pl.when(step == 0)
    def _():
        pltpu.make_async_copy(bank.at[slots[bank.shape[0] - 1]], last, sem).start()

    hidden = tokens[...].astype(jnp.float32)
    scale = lax.rsqrt(jnp.mean(hidden * hidden, axis=-1, keepdims=True) + 1e-06)
    normed[...] = (hidden * scale).astype(jnp.bfloat16)

    @pl.when(step == pl.num_programs(0) - 1)
    def _():
        pltpu.make_async_copy(last, last, sem).wait()


def prepare(slots, bank, tokens):
    rows = pl.BlockSpec((tokens.shape[0] // 2, tokens.shape[1]), lambda i, *_: (i, 0))
    return pl.pallas_call(
        prepare_kernel,
        out_shape=(
            jax.ShapeDtypeStruct(tokens.shape, jnp.bfloat16),
            jax.ShapeDtypeStruct(bank.shape[1:], jnp.bfloat16),
        ),
        grid_spec=pltpu.PrefetchScalarGridSpec(
            num_scalar_prefetch=1,
            grid=(2,),
            in_specs=[pl.BlockSpec(memory_space=pl.ANY), rows],
            out_specs=[rows, pl.BlockSpec(bank.shape[1:], lambda i, *_: (0, 0))],
            scratch_shapes=[pltpu.SemaphoreType.DMA],
        ),
        cost_estimate=pl.CostEstimate(flops=2**30, bytes_accessed=2**23, transcendentals=0),
        name="prepare",
    )(slots, bank, tokens)


def pack_kernel(at, heads, *refs):
    ins, (out, sem) = refs[:-2], refs[-2:]
    for i in range(3):
        for h in range(heads):
            cols = pl.ds((at + h) * HEAD_DIM, HEAD_DIM)
            pltpu.make_async_copy(ins[i].at[:, cols], out.at[i * heads + h], sem).start()
    if len(ins) > 3:
        for i in range(out.shape[0] - 3 * heads):
            rows = pl.ds(i * HEAD_DIM, HEAD_DIM)
            pltpu.make_async_copy(ins[3].at[rows], out.at[3 * heads + i], sem).start()
    pltpu.make_async_copy(out, out, sem).wait()


def pack(weights, at, heads, *tail):
    count = 3 * heads + sum(t.shape[0] // HEAD_DIM for t in tail)
    return pl.pallas_call(
        functools.partial(pack_kernel, at, heads),
        out_shape=jax.ShapeDtypeStruct((count, weights[0].shape[0], HEAD_DIM), jnp.bfloat16),
        in_specs=[pl.BlockSpec(memory_space=pl.ANY)] * (3 + len(tail)),
        out_specs=pl.BlockSpec(memory_space=pltpu.VMEM),
        scratch_shapes=[pltpu.SemaphoreType.DMA],
        name="pack",
    )(*weights, *tail)


def origins(me):
    x_lo, z, c = me // (Z * CORE), (me // CORE) % Z, me % CORE
    found = []
    for core in (c, 1 - c):
        for x in (x_lo, 1 - x_lo):
            for dz in (0, 3, 1, 2):
                found.append((x * Z + (z + dz) % Z) * CORE + core)
    return jnp.stack(found).astype(jnp.int32)


def only_head(q, h, heads):
    empty = jnp.zeros((q.shape[0], HEAD_DIM), q.dtype)
    return jnp.concatenate(
        [q[:, i * HEAD_DIM : (i + 1) * HEAD_DIM] if i == h else empty for i in range(heads)], axis=1
    )


def attend_kernel(heads, first, group, skip, slots, rows, bank, normed, *rest):
    arrived, rest = (rest[0], rest[1:]) if first == 0 else (None, rest)
    pieces, out, ctx, w, x, ctx_sem, w_sem, x_sem = rest[:8], *rest[8 + skip :]
    step, steps = pl.program_id(0), pl.num_programs(0)
    width = heads * HEAD_DIM
    kv_rows = bank.shape[1]
    shard = pieces[0].shape[2]
    block = normed.shape[0] // bank.shape[0]
    tall = group * block

    def fetch_tokens(g, slot):
        at = pl.multiple_of(first * block + g * tall, tall)
        pltpu.make_async_copy(normed.at[pl.ds(at, tall)], x.at[slot], x_sem.at[slot]).start()

    def fetch(g, slot, j):
        c = first + g * group + j
        dst = ctx.at[slot, pl.ds(j * kv_rows, kv_rows), :]
        sem = ctx_sem.at[slot, j]
        if first == 0 and j == 0:

            @pl.when(g == 0)
            def _():
                pltpu.make_async_copy(arrived, dst, sem).start()

            @pl.when(g > 0)
            def _():
                pltpu.make_async_copy(bank.at[slots[jnp.maximum(c - 1, 0)]], dst, sem).start()
        else:
            pltpu.make_async_copy(bank.at[slots[c - 1]], dst, sem).start()

    def fetch_next():
        @pl.when(step + 1 < steps)
        def _():
            fetch_tokens(step + 1, (step + 1) % 2)
            for j in range(group):
                fetch(step + 1, (step + 1) % 2, j)

    @pl.when(step == 0)
    def _():
        for i in range(8):
            for k in range(2):
                at = pl.multiple_of(rows[i * 2 + k] * shard, shard)
                pltpu.make_async_copy(
                    pieces[i].at[k, pl.ds(0, 3 * heads)], w.at[:, pl.ds(at, shard), :], w_sem
                ).start()
        fetch_tokens(0, 0)
        fetch(0, 0, 0)

    slot = step % 2

    def compute(starting):
        if starting:
            pltpu.make_async_copy(w, w, w_sem).wait()
            for j in range(1, group):
                fetch(0, 0, j)
        else:
            fetch_next()
        pltpu.make_async_copy(x.at[slot], x.at[slot], x_sem.at[slot]).wait()
        blocks = [ctx.at[slot, pl.ds(j * kv_rows, kv_rows)] for j in range(group)]
        if not starting:
            for j in range(group):
                pltpu.make_async_copy(blocks[j], blocks[j], ctx_sem.at[slot, j]).wait()
        wq = jnp.concatenate([w[i] for i in range(heads)], axis=1)
        wkv = jnp.concatenate([w[i] for i in range(heads, 3 * heads)], axis=1)
        q = jnp.dot(x[slot], wq, preferred_element_type=jnp.float32).astype(jnp.bfloat16)
        kv, weights = {}, {}
        for j in range(group + 2 * LAG):
            if j < group:
                if starting:
                    pltpu.make_async_copy(blocks[j], blocks[j], ctx_sem.at[slot, j]).wait()
                    if j == AHEAD:
                        fetch_next()
                kv[j] = jnp.dot(blocks[j][...], wkv, preferred_element_type=jnp.float32).astype(jnp.bfloat16)
            i = j - LAG
            if 0 <= i < group:
                qi = q[i * block : (i + 1) * block]
                stacked = jnp.concatenate([only_head(qi, h, heads) for h in range(heads)], axis=0)
                s = lax.dot_general(
                    stacked, kv[i][:, :width], (((1,), (1,)), ((), ())), preferred_element_type=jnp.float32
                )
                s = s * (1.0 / math.sqrt(HEAD_DIM))
                e = jnp.exp(s - jnp.max(s, axis=-1, keepdims=True))
                weights[i] = (e / jnp.sum(e, axis=-1, keepdims=True)).astype(jnp.bfloat16)
            i = j - 2 * LAG
            if 0 <= i < group:
                o = jnp.dot(weights[i], kv[i][:, width:], preferred_element_type=jnp.float32).astype(jnp.bfloat16)
                for h in range(heads):
                    cols = slice(h * HEAD_DIM, (h + 1) * HEAD_DIM)
                    out[i * block : (i + 1) * block, cols] = o[h * block : (h + 1) * block, cols]

    @pl.when(step == 0)
    def _():
        compute(True)

    @pl.when(step > 0)
    def _():
        compute(False)


def attend(slots, rows, bank, arrived, normed, pieces, heads, first, blocks, group, whole=False, into=None):
    model = normed.shape[1]
    kv_rows = bank.shape[1]
    arrived = [arrived] if first == 0 else []
    into = [] if into is None else [into]
    at = first // group if whole else 0
    block = normed.shape[0] // bank.shape[0]
    width = heads * HEAD_DIM
    hbm = pl.BlockSpec(memory_space=pltpu.HBM)
    flops = 2 * blocks * (2 * kv_rows + block) * model * width
    return pl.pallas_call(
        functools.partial(attend_kernel, heads, first, group, len(into)),
        out_shape=jax.ShapeDtypeStruct((normed.shape[0] if whole else blocks * block, width), jnp.bfloat16),
        grid_spec=pltpu.PrefetchScalarGridSpec(
            num_scalar_prefetch=2,
            grid=(blocks // group,),
            in_specs=[hbm] * (2 + len(arrived) + 8 + len(into)),
            out_specs=pl.BlockSpec((group * block, width), lambda i, *_: (at + i, 0)),
            scratch_shapes=[
                pltpu.VMEM((2, group * kv_rows, model), jnp.bfloat16),
                pltpu.VMEM((3 * heads, model, HEAD_DIM), jnp.bfloat16),
                pltpu.VMEM((2, group * block, model), jnp.bfloat16),
                pltpu.SemaphoreType.DMA((2, group)),
                pltpu.SemaphoreType.DMA,
                pltpu.SemaphoreType.DMA((2,)),
            ],
        ),
        input_output_aliases={4 + len(arrived) + 8: 0} if into else {},
        cost_estimate=pl.CostEstimate(
            flops=flops, bytes_accessed=2 * blocks * kv_rows * model, transcendentals=0
        ),
        compiler_params=pltpu.CompilerParams(vmem_limit_bytes=60 * 2**20),
        name="attend",
    )(slots, rows, bank, normed, *arrived, *pieces, *into)


def load_parts(parts, cols, att, start, sem):
    tall, width = parts[0].shape
    for k in range(4):
        c = pl.multiple_of(cols[k] * width, width)
        pltpu.make_async_copy(parts[k], att.at[pl.ds(start, tall), pl.ds(c, width)], sem).start()


def project_first_kernel(rows, cols, *refs):
    parts, pieces = refs[:4], refs[4:12]
    out, w_next, w, att, att_sem, w_sem, next_sem = refs[12:]
    deep, wide = w.shape[0] // 4, w.shape[1] // 4
    tile = pieces[0].shape[2]
    count = deep // tile
    lead = pieces[0].shape[1] - 2 * count
    load_parts(parts, cols, att, 0, att_sem)
    for dst, sem, at in ((w, w_sem, lead), (w_next, next_sem, lead + count)):
        for i in range(8):
            for k in range(2):
                origin = rows[i * 2 + k]
                r = pl.multiple_of((origin // 4) * deep, deep)
                c = pl.multiple_of((origin % 4) * wide, wide)
                for t in range(count):
                    pltpu.make_async_copy(
                        pieces[i].at[k, at + t], dst.at[pl.ds(r + t * tile, tile), pl.ds(c, wide)], sem
                    ).start()
    pltpu.make_async_copy(att, att, att_sem).wait()
    pltpu.make_async_copy(w, w, w_sem).wait()
    out[...] = jnp.dot(att[...], w[...], preferred_element_type=jnp.float32)
    pltpu.make_async_copy(w_next, w_next, next_sem).wait()


def project_first(rows, cols, parts, pieces, wide):
    tall, deep = parts[0].shape[0], 4 * parts[0].shape[1]
    hbm = pl.BlockSpec(memory_space=pltpu.HBM)
    return pl.pallas_call(
        project_first_kernel,
        out_shape=(jax.ShapeDtypeStruct((tall, wide), jnp.float32), jax.ShapeDtypeStruct((deep, wide), jnp.bfloat16)),
        grid_spec=pltpu.PrefetchScalarGridSpec(
            num_scalar_prefetch=2,
            grid=(1,),
            in_specs=[hbm] * 12,
            out_specs=(
                pl.BlockSpec((tall, wide), lambda i, *_: (0, 0)),
                pl.BlockSpec((deep, wide), lambda i, *_: (0, 0)),
            ),
            scratch_shapes=[
                pltpu.VMEM((deep, wide), jnp.bfloat16),
                pltpu.VMEM((tall, deep), jnp.bfloat16),
                pltpu.SemaphoreType.DMA,
                pltpu.SemaphoreType.DMA,
                pltpu.SemaphoreType.DMA,
            ],
        ),
        compiler_params=pltpu.CompilerParams(vmem_limit_bytes=60 * 2**20),
        cost_estimate=pl.CostEstimate(flops=2 * tall * deep * wide, bytes_accessed=2**23, transcendentals=0),
        name="project_first",
    )(rows, cols, *parts, *pieces)


def project_last_kernel(starts, cols, *refs):
    n = 4 * len(starts)
    parts, (w_in, share_in, out, w, share, att, w_sem, sem, att_sem) = refs[:n], refs[n:]
    pltpu.make_async_copy(w_in, w, w_sem).start()
    for i, start in enumerate(starts):
        load_parts(parts[4 * i : 4 * i + 4], cols, att, start, att_sem)
    pltpu.make_async_copy(share_in, share, sem).start()
    pltpu.make_async_copy(w, w, w_sem).wait()
    pltpu.make_async_copy(att, att, att_sem).wait()
    pltpu.make_async_copy(share, share, sem).wait()
    rest = jnp.dot(att[...], w[...], preferred_element_type=jnp.float32)
    out[...] = (share[...] + rest).astype(jnp.bfloat16)


def project_last(cols, runs, weights, share):
    (tall, wide), deep = share.shape, weights.shape[0]
    hbm = pl.BlockSpec(memory_space=pltpu.HBM)
    starts = tuple(start for start, _ in runs)
    parts = [p for _, four in runs for p in four]
    return pl.pallas_call(
        functools.partial(project_last_kernel, starts),
        out_shape=jax.ShapeDtypeStruct((tall, wide), jnp.bfloat16),
        grid_spec=pltpu.PrefetchScalarGridSpec(
            num_scalar_prefetch=1,
            grid=(1,),
            in_specs=[hbm] * (len(parts) + 2),
            out_specs=pl.BlockSpec((tall, wide), lambda i, *_: (0, 0)),
            scratch_shapes=[
                pltpu.VMEM((deep, wide), jnp.bfloat16),
                pltpu.VMEM((tall, wide), jnp.float32),
                pltpu.VMEM((tall, deep), jnp.bfloat16),
                pltpu.SemaphoreType.DMA,
                pltpu.SemaphoreType.DMA,
                pltpu.SemaphoreType.DMA,
            ],
        ),
        compiler_params=pltpu.CompilerParams(vmem_limit_bytes=60 * 2**20),
        cost_estimate=pl.CostEstimate(flops=2 * tall * deep * wide, bytes_accessed=2**23, transcendentals=0),
        name="project_last",
    )(cols, *parts, weights, share)


def local(tokens, neighbor_bank, slots, w_query, w_key, w_value, w_out):
    blocks = neighbor_bank.shape[0]
    me, head_at = lax.axis_index("seq"), lax.axis_index("head")
    rows = origins(me)
    cols = jnp.stack([(head_at + d) % 4 for d in (0, 3, 1, 2)]).astype(jnp.int32)

    swap = [
        ((4 * a + j) * 4 + b, (4 * b + j) * 4 + a) for a in range(4) for b in range(4) for j in range(4)
    ]
    weights = (w_query, w_key, w_value)
    z_first = gather_z(pack(weights, 0, CHUNK_HEADS[0]))
    out_shard = lax.ppermute(w_out, ("seq", "head"), swap)
    normed, last = prepare(slots, neighbor_bank, tokens)

    x_first = gather_x(z_first)
    second = pack(weights, CHUNK_HEADS[0], CHUNK_HEADS[1], out_shard)
    z_second = gather_z(after(second, *z_first))
    devices = lax.axis_size("seq")
    arrived = lax.ppermute(last, "seq", [(i, i + 1) for i in range(devices - 1)])
    pieces = gather_core(x_first)

    block = tokens.shape[0] // blocks
    ring = lambda block, d: lax.ppermute(block, "head", [(i, (i + d) % 4) for i in range(4)])

    def exchange(own):
        return [own, ring(own, 1), ring(own, -1), ring(own, 2)]

    heads, x, own = CHUNK_HEADS[0], normed, None
    for n, (start, count) in enumerate(RUNS):
        own = attend(slots, rows, neighbor_bank, arrived, x, pieces, heads, start, count, GROUP, whole=True, into=own)
        x = after(normed, own)
        if n == 0:
            x_second = gather_x([after(p, own) for p in z_second])
    pieces = gather_core(x_second)
    first_parts = exchange(own)

    heads, runs = CHUNK_HEADS[1], []
    for n, (start, count) in enumerate(RUNS[::-1], 2):
        own = attend(slots, rows, neighbor_bank, arrived, x, pieces, heads, start, count, GROUP)
        x = after(normed, own)
        runs.append((start * block, exchange(own)))
    share, weights = project_first(rows, cols, first_parts, pieces, w_out.shape[0])
    return project_last(cols, runs, weights, share)


def solution(mesh):
    in_specs = (
        P(("batch", "seq"), None),
        P(("batch", "seq"), None, None),
        P(("batch", "seq")),
        P("seq", "head"),
        P("seq", "head"),
        P("seq", "head"),
        P("head", "seq"),
    )
    out_specs = P(("batch", "seq"), "head")

    return jax.shard_map(local, mesh=mesh, in_specs=in_specs, out_specs=out_specs, check_vma=False)
```

time: 171 us -> 169 us (0.988)
  the two profiles are of different devices: /device:TPU:8 before, /device:TPU:3 now
where the time goes in v1:
time: 169 us; the launch traced here: 168 us
  Pallas kernels  64.7 us (38%)
  waiting for transfers between devices  50.9 us (30%)
  starting transfers between devices  43.4 us (26%)
  local copies, waits for them, and re-layouts  3.9 us (2%)
  other arithmetic  3.81 us (2%)
    pallas_call x4, Pallas kernels, attend(): pl.pallas_call(functools.partial(attend_kernel, heads, first, group, len(...  44.9 us
    ppermute x18, waiting for transfers between devices, plane(): return lax.ppermute(block, ('seq', 'batch'), pairs)  32.7 us
    ppermute x18, starting transfers between devices, plane(): return lax.ppermute(block, ('seq', 'batch'), pairs)  21.2 us
    ppermute x9, waiting for transfers between devices, local(): lax.ppermute(block, 'head', [(i, (i + d) % 4) for i in range(4)])  12.7 us
    ppermute x9, starting transfers between devices, local(): lax.ppermute(block, 'head', [(i, (i + d) % 4) for i in range(4)])  12.4 us
    pallas_call x1, Pallas kernels, project_first(): pl.pallas_call(project_first_kernel, out_shape=(jax.ShapeDtypeStruct((tal...  5.88 us
    ppermute x1, waiting for transfers between devices, local(): out_shard = lax.ppermute(w_out, ('seq', 'head'), swap)  5.49 us
    pallas_call x1, Pallas kernels, project_last(): pl.pallas_call(functools.partial(project_last_kernel, starts), out_shape=...  5.46 us
  transfers between devices with their start and end apart: 29, of which 8 were waited for; matrix products, arithmetic and copies ran while one was open for 3% of the time, Pallas kernels for 34%

profile of v1, /device:TPU:3, one launch (start us, length us, event | category | flops | bytes accessed | tf_op | source)
XLA Modules:
  0.0 167.6 jit_solution(12622531337940350138)
XLA Ops:
  3.2 2.2 %collective-permute-start.1 = (bf16[6,128,128]{2,1,0:T(8,128)(2,1)}, bf16[6,128,128]{2,1,0:T(8,128)(2,1)S(1)}, u32[]{:S(2)}, u32[]{:S(2)}) collective-permute-start(bf16[6,128,128]{2,1,0:T(8,128)(2,1)} %pack.2), channel_id=1, source_target_pairs={{0,48},{8,56},{16,0},{24,8},{32,16},{40,24},{48,32},{56,40},{64,11... | collective-permute-start | bytes 589832 | tf_op jit(solution)/shard_map/ppermute | solution.py:42
  6.7 3.5 %collective-permute-done = bf16[6,128,128]{2,1,0:T(8,128)(2,1)S(1)} collective-permute-done((bf16[6,128,128]{2,1,0:T(8,128)(2,1)}, bf16[6,128,128]{2,1,0:T(8,128)(2,1)S(1)}, u32[]{:S(2)}, u32[]{:S(2)}) %collective-permute-start) | collective-permute-done | bytes 196640 | tf_op jit(solution)/shard_map/ppermute | solution.py:42
  12.4 2.8 %collective-permute-done.2 = bf16[6,128,128]{2,1,0:T(8,128)(2,1)S(1)} collective-permute-done((bf16[6,128,128]{2,1,0:T(8,128)(2,1)}, bf16[6,128,128]{2,1,0:T(8,128)(2,1)S(1)}, u32[]{:S(2)}, u32[]{:S(2)}) %collective-permute-start.2) | collective-permute-done | bytes 196640 | tf_op jit(solution)/shard_map/ppermute | solution.py:42
  17.5 3.2 %collective-permute-done.3.rest_2_.rest_3_ = bf16[2,6,128,128]{3,2,1,0:T(8,128)(2,1)S(1)} collective-permute-done((bf16[2,6,128,128]{3,2,1,0:T(8,128)(2,1)S(1)}, bf16[2,6,128,128]{3,2,1,0:T(8,128)(2,1)S(1)}, u32[]{:S(2)}, u32[]{:S(2)}) %collective-permute-start.3) | collective-permute-done | bytes 393248 | tf_op jit(solution)/shard_map/ppermute | solution.py:42
  20.6 2.1 %collective-permute-start.7 = (bf16[2,6,128,128]{3,2,1,0:T(8,128)(2,1)S(1)}, bf16[2,6,128,128]{3,2,1,0:T(8,128)(2,1)S(1)}, u32[]{:S(2)}, u32[]{:S(2)}) collective-permute-start(bf16[2,6,128,128]{3,2,1,0:T(8,128)(2,1)S(1)} %collective-permute-done.3.rest_2_.rest_3_), channel_id=1, source_target_pairs={{0,8},{8,0},{16,24},{24,16},{32,40},{40,32},{48,56},{56,48},{64,72... | collective-permute-start | bytes 1179656 | tf_op jit(solution)/shard_map/ppermute | solution.py:42
  24.6 2.4 %collective-permute-start.8 = (bf16[2,6,128,128]{3,2,1,0:T(8,128)(2,1)S(1)}, bf16[2,6,128,128]{3,2,1,0:T(8,128)(2,1)S(1)}, u32[]{:S(2)}, u32[]{:S(2)}) collective-permute-start(bf16[2,6,128,128]{3,2,1,0:T(8,128)(2,1)S(1)} %collective-permute-done.4.rest_3_.rest_4_), channel_id=1, source_target_pairs={{0,8},{8,0},{16,24},{24,16},{32,40},{40,32},{48,56},{56,48},{64,72... | collective-permute-start | bytes 1179656 | tf_op jit(solution)/shard_map/ppermute | solution.py:42
  26.9 5.1 %collective-permute-start.10 = (bf16[512,128]{1,0:T(8,128)(2,1)}, bf16[512,128]{1,0:T(8,128)(2,1)S(1)}, u32[]{:S(2)}, u32[]{:S(2)}) collective-permute-start(bf16[512,128]{1,0:T(8,128)(2,1)} %param.13), channel_id=1, source_target_pairs={{0,0},{8,8},{16,16},{24,24},{2,32},{10,40},{18,48},{26,56},{4,64},... | collective-permute-start | bytes 393224 | tf_op jit(solution)/shard_map/ppermute | solution.py:389
  32.7 5.5 %collective-permute-done.10.refs_3_ = bf16[512,128]{1,0:T(8,128)(2,1)S(1)} collective-permute-done((bf16[512,128]{1,0:T(8,128)(2,1)}, bf16[512,128]{1,0:T(8,128)(2,1)S(1)}, u32[]{:S(2)}, u32[]{:S(2)}) %collective-permute-start.10) | collective-permute-done | bytes 131104 | tf_op jit(solution)/shard_map/ppermute | solution.py:389
  40.5 3.1 %collective-permute-start.13 = (bf16[10,128,128]{2,1,0:T(8,128)(2,1)}, bf16[10,128,128]{2,1,0:T(8,128)(2,1)S(1)}, u32[]{:S(2)}, u32[]{:S(2)}) collective-permute-start(bf16[10,128,128]{2,1,0:T(8,128)(2,1)} %pack.3), channel_id=1, source_target_pairs={{0,32},{8,40},{16,48},{24,56},{32,0},{40,8},{48,16},{56,24},{64,96... | collective-permute-start | bytes 983048 | tf_op jit(solution)/shard_map/ppermute | solution.py:42
  45.1 5.3 %prepare.1 = (bf16[1024,2048]{1,0:T(8,128)(2,1)}, bf16[256,2048]{1,0:T(8,128)(2,1)}) custom-call(s32[16]{0:T(128)} %slots.9, bf16[16,256,2048]{2,1,0:T(8,128)(2,1)} %bank.9, bf16[1024,2048]{1,0:T(8,128)(2,1)} %tokens.1), custom_call_target="tpu_custom_call" | custom-call | flops 1073741824 | bytes 8388608 | tf_op jit(solution)/shard_map/prepare/pallas_call | solution.py:82
  50.5 4.8 %collective-permute-start.9 = (bf16[256,2048]{1,0:T(8,128)(2,1)}, bf16[256,2048]{1,0:T(8,128)(2,1)}, u32[]{:S(2)}, u32[]{:S(2)}) collective-permute-start(bf16[256,2048]{1,0:T(8,128)(2,1)} %get-tuple-element.19), channel_id=1, source_target_pairs={{0,8},{8,16},{16,24},{24,32},{32,40},{40,48},{48,56},{56,64},{64,7... | collective-permute-start | bytes 3145736 | tf_op jit(solution)/shard_map/ppermute | solution.py:396
  56.1 8.2 %attend.4.rest_9_ = bf16[1024,256]{1,0:T(8,128)(2,1)} custom-call(s32[16]{0:T(128)} %slots.9, s32[16]{0:T(128)} %stack.123.rows, bf16[16,256,2048]{2,1,0:T(8,128)(2,1)} %bank.9, bf16[1024,2048]{1,0:T(8,128)(2,1)} %get-tuple-element.26.normed, bf16[2,6,128,128]{3,2,1,0:T(8,128)(2,1)} %copy-done.5, bf16[2,6,128,128]{3,2,1,0:T(8,128)(2,1)} %copy-done.6, ...), custom_call_target="tpu_custom_call" | custom-call | flops 2415919104 | bytes 4194304 | tf_op jit(solution)/shard_map/attend/pallas_call | solution.py:251
  68.6 13.5 %collective-permute-done.14.rest_3_.rest_2_.refs_6_ = bf16[2,10,128,128]{3,2,1,0:T(8,128)(2,1)S(1)} collective-permute-done((bf16[2,10,128,128]{3,2,1,0:T(8,128)(2,1)S(1)}, bf16[2,10,128,128]{3,2,1,0:T(8,128)(2,1)S(1)}, u32[]{:S(2)}, u32[]{:S(2)}) %collective-permute-start.14) | collective-permute-done | bytes 655392 | tf_op jit(solution)/shard_map/ppermute | solution.py:42
  82.4 7.8 %collective-permute-done.15.rest_4_.rest_3_.refs_7_ = bf16[2,10,128,128]{3,2,1,0:T(8,128)(2,1)S(1)} collective-permute-done((bf16[2,10,128,128]{3,2,1,0:T(8,128)(2,1)S(1)}, bf16[2,10,128,128]{3,2,1,0:T(8,128)(2,1)S(1)}, u32[]{:S(2)}, u32[]{:S(2)}) %collective-permute-start.15) | collective-permute-done | bytes 655392 | tf_op jit(solution)/shard_map/ppermute | solution.py:42
  91.6 14.3 %attend.5.refs_0_ = bf16[1024,256]{1,0:T(8,128)(2,1)} custom-call(s32[16]{0:T(128)} %slots.9, s32[16]{0:T(128)} %stack.123.rows, bf16[16,256,2048]{2,1,0:T(8,128)(2,1)} %bank.9, bf16[1024,2048]{1,0:T(8,128)(2,1)} %get-tuple-element.26.normed, bf16[256,2048]{1,0:T(8,128)(2,1)} %collective-permute-done.9.rest_0_, ...), custom_call_target="tpu_custom_call", output_to_operand_aliasing={{}: (13, {})} | custom-call | flops 7247757312 | bytes 12582912 | tf_op jit(solution)/shard_map/attend/pallas_call | solution.py:251
  105.9 2.0 %collective-permute-start.26 = (bf16[1024,256]{1,0:T(8,128)(2,1)}, bf16[1024,256]{1,0:T(8,128)(2,1)S(1)}, u32[]{:S(2)}, u32[]{:S(2)}) collective-permute-start(bf16[1024,256]{1,0:T(8,128)(2,1)} %attend.5.refs_0_), channel_id=1, source_target_pairs={{0,2},{2,4},{4,6},{6,0},{1,3},{3,5},{5,7},{7,1},{8,10},{10,12},{12... | collective-permute-start | bytes 1572872 | tf_op jit(solution)/shard_map/ppermute | solution.py:400
  109.8 14.3 %attend.6.refs_0_ = bf16[768,256]{1,0:T(8,128)(2,1)} custom-call(s32[16]{0:T(128)} %slots.9, s32[16]{0:T(128)} %stack.123.rows, bf16[16,256,2048]{2,1,0:T(8,128)(2,1)} %bank.9, bf16[1024,2048]{1,0:T(8,128)(2,1)} %get-tuple-element.26.normed, bf16[256,2048]{1,0:T(8,128)(2,1)} %collective-permute-done.9.rest_0_, bf16[2,10,128,128]{3,2,1,0:T(8,128)(2,1)} %copy-done, ...), custom_call_target="tpu_custom_call" | custom-call | flops 7247757312 | bytes 12582912 | tf_op jit(solution)/shard_map/attend/pallas_call | solution.py:251
  124.2 2.7 %collective-permute-start.21 = (bf16[768,256]{1,0:T(8,128)(2,1)}, bf16[768,256]{1,0:T(8,128)(2,1)S(1)}, u32[]{:S(2)}, u32[]{:S(2)}) collective-permute-start(bf16[768,256]{1,0:T(8,128)(2,1)} %attend.6.refs_0_), channel_id=1, source_target_pairs={{0,6},{2,0},{4,2},{6,4},{1,7},{3,1},{5,3},{7,5},{8,14},{10,8},{12,... | collective-permute-start | bytes 1179656 | tf_op jit(solution)/shard_map/ppermute | solution.py:400
  127.5 8.1 %attend.7.refs_4_ = bf16[256,256]{1,0:T(8,128)(2,1)} custom-call(s32[16]{0:T(128)} %slots.9, s32[16]{0:T(128)} %stack.123.rows, bf16[16,256,2048]{2,1,0:T(8,128)(2,1)} %bank.9, bf16[1024,2048]{1,0:T(8,128)(2,1)} %get-tuple-element.26.normed, bf16[2,10,128,128]{3,2,1,0:T(8,128)(2,1)} %copy-done, bf16[2,10,128,128]{3,2,1,0:T(8,128)(2,1)} %copy-done.1, ...), custom_call_target="tpu_custom_call" | custom-call | flops 2415919104 | bytes 4194304 | tf_op jit(solution)/shard_map/attend/pallas_call | solution.py:251
  137.1 2.0 %collective-permute-start.24 = (bf16[256,256]{1,0:T(8,128)(2,1)}, bf16[256,256]{1,0:T(8,128)(2,1)S(1)}, u32[]{:S(2)}, u32[]{:S(2)}) collective-permute-start(bf16[256,256]{1,0:T(8,128)(2,1)} %attend.7.refs_4_), channel_id=1, source_target_pairs={{0,6},{2,0},{4,2},{6,4},{1,7},{3,1},{5,3},{7,5},{8,14},{10,8},{12,... | collective-permute-start | bytes 393224 | tf_op jit(solution)/shard_map/ppermute | solution.py:400
  139.1 12.7 %collective-permute-done.23.refs_5_ = bf16[256,256]{1,0:T(8,128)(2,1)S(1)} collective-permute-done((bf16[256,256]{1,0:T(8,128)(2,1)}, bf16[256,256]{1,0:T(8,128)(2,1)S(1)}, u32[]{:S(2)}, u32[]{:S(2)}) %collective-permute-start.23) | collective-permute-done | bytes 131104 | tf_op jit(solution)/shard_map/ppermute | solution.py:400
  151.8 2.5 %collective-permute-start.25 = (bf16[256,256]{1,0:T(8,128)(2,1)}, bf16[256,256]{1,0:T(8,128)(2,1)S(1)}, u32[]{:S(2)}, u32[]{:S(2)}) collective-permute-start(bf16[256,256]{1,0:T(8,128)(2,1)} %attend.7.refs_4_), channel_id=1, source_target_pairs={{0,4},{2,6},{4,0},{6,2},{1,5},{3,7},{5,1},{7,3},{8,12},{10,14},{12... | collective-permute-start | bytes 393224 | tf_op jit(solution)/shard_map/ppermute | solution.py:400
  154.9 5.9 %project_first.1 = (f32[1024,512]{1,0:T(8,128)}, bf16[1024,512]{1,0:T(8,128)(2,1)}) custom-call(s32[16]{0:T(128)} %stack.123.rows, s32[4]{0:T(128)} %pad_add_fusion.cols, bf16[1024,256]{1,0:T(8,128)(2,1)} %attend.5.refs_0_, bf16[1024,256]{1,0:T(8,128)(2,1)} %copy-done.8, bf16[1024,256]{1,0:T(8,128)(2,1)} %copy-done.9, bf16[1024,256]{1,0:T(8,128)(2,1)} %copy-done.10, ...), custom_call_target="tpu_custom_call" | custom-call | flops 1073741824 | bytes 8388608 | tf_op jit(solution)/shard_map/project_first/pallas_call | solution.py:311
  161.9 5.5 %project_last.1 = bf16[1024,512]{1,0:T(8,128)(2,1)} custom-call(s32[4]{0:T(128)} %pad_add_fusion.cols, bf16[768,256]{1,0:T(8,128)(2,1)} %attend.6.refs_0_, bf16[768,256]{1,0:T(8,128)(2,1)} %copy-done.11, bf16[768,256]{1,0:T(8,128)(2,1)} %copy-done.12, bf16[768,256]{1,0:T(8,128)(2,1)} %copy-done.13, bf16[256,256]{1,0:T(8,128)(2,1)} %attend.7.refs_4_, ...), custom_call_target="tpu_custom_call" | custom-call | flops 1073741824 | bytes 8388608 | tf_op jit(solution)/shard_map/project_last/pallas_call | solution.py:355
  (97 shorter events, 27.4 us)
Async XLA Ops:
  5.4 9.8 %collective-permute-start.2 = (bf16[6,128,128]{2,1,0:T(8,128)(2,1)}, bf16[6,128,128]{2,1,0:T(8,128)(2,1)S(1)}, u32[]{:S(2)}, u32[]{:S(2)}) collective-permute-start(bf16[6,128,128]{2,1,0:T(8,128)(2,1)} %pack.2), channel_id=1, source_target_pairs={{0,32},{8,40},{16,48},{24,56},{32,0},{40,8},{48,16},{56,24},{64,96... | collective-permute-start | bytes 589832 | tf_op jit(solution)/shard_map/ppermute | solution.py:42
  15.7 28.0 %collective-permute-start.5 = (bf16[2,6,128,128]{3,2,1,0:T(8,128)(2,1)S(1)}, bf16[2,6,128,128]{3,2,1,0:T(8,128)(2,1)S(1)}, u32[]{:S(2)}, u32[]{:S(2)}) collective-permute-start(bf16[2,6,128,128]{3,2,1,0:T(8,128)(2,1)S(1)} %pad_maximum_fusion.2.rest_0_.rest_1_), channel_id=1, source_target_pairs={{0,8},{8,0},{16,24},{24,16},{32,40},{40,32},{48,56},{56,48},{64,72... | collective-permute-start | bytes 1179656 | tf_op jit(solution)/shard_map/ppermute | solution.py:42
  17.5 26.7 %collective-permute-start.6 = (bf16[2,6,128,128]{3,2,1,0:T(8,128)(2,1)S(1)}, bf16[2,6,128,128]{3,2,1,0:T(8,128)(2,1)S(1)}, u32[]{:S(2)}, u32[]{:S(2)}) collective-permute-start(bf16[2,6,128,128]{3,2,1,0:T(8,128)(2,1)S(1)} %pad_maximum_fusion.3.rest_1_.rest_2_), channel_id=1, source_target_pairs={{0,8},{8,0},{16,24},{24,16},{32,40},{40,32},{48,56},{56,48},{64,72... | collective-permute-start | bytes 1179656 | tf_op jit(solution)/shard_map/ppermute | solution.py:42
  20.6 29.9 %collective-permute-start.7 = (bf16[2,6,128,128]{3,2,1,0:T(8,128)(2,1)S(1)}, bf16[2,6,128,128]{3,2,1,0:T(8,128)(2,1)S(1)}, u32[]{:S(2)}, u32[]{:S(2)}) collective-permute-start(bf16[2,6,128,128]{3,2,1,0:T(8,128)(2,1)S(1)} %collective-permute-done.3.rest_2_.rest_3_), channel_id=1, source_target_pairs={{0,8},{8,0},{16,24},{24,16},{32,40},{40,32},{48,56},{56,48},{64,72... | collective-permute-start | bytes 1179656 | tf_op jit(solution)/shard_map/ppermute | solution.py:42
  24.6 30.8 %collective-permute-start.8 = (bf16[2,6,128,128]{3,2,1,0:T(8,128)(2,1)S(1)}, bf16[2,6,128,128]{3,2,1,0:T(8,128)(2,1)S(1)}, u32[]{:S(2)}, u32[]{:S(2)}) collective-permute-start(bf16[2,6,128,128]{3,2,1,0:T(8,128)(2,1)S(1)} %collective-permute-done.4.rest_3_.rest_4_), channel_id=1, source_target_pairs={{0,8},{8,0},{16,24},{24,16},{32,40},{40,32},{48,56},{56,48},{64,72... | collective-permute-start | bytes 1179656 | tf_op jit(solution)/shard_map/ppermute | solution.py:42
  26.9 11.3 %collective-permute-start.10 = (bf16[512,128]{1,0:T(8,128)(2,1)}, bf16[512,128]{1,0:T(8,128)(2,1)S(1)}, u32[]{:S(2)}, u32[]{:S(2)}) collective-permute-start(bf16[512,128]{1,0:T(8,128)(2,1)} %param.13), channel_id=1, source_target_pairs={{0,0},{8,8},{16,16},{24,24},{2,32},{10,40},{18,48},{26,56},{4,64},... | collective-permute-start | bytes 393224 | tf_op jit(solution)/shard_map/ppermute | solution.py:389
  40.5 23.8 %collective-permute-start.13 = (bf16[10,128,128]{2,1,0:T(8,128)(2,1)}, bf16[10,128,128]{2,1,0:T(8,128)(2,1)S(1)}, u32[]{:S(2)}, u32[]{:S(2)}) collective-permute-start(bf16[10,128,128]{2,1,0:T(8,128)(2,1)} %pack.3), channel_id=1, source_target_pairs={{0,32},{8,40},{16,48},{24,56},{32,0},{40,8},{48,16},{56,24},{64,96... | collective-permute-start | bytes 983048 | tf_op jit(solution)/shard_map/ppermute | solution.py:42
  43.7 20.7 %collective-permute-start.12 = (bf16[10,128,128]{2,1,0:T(8,128)(2,1)}, bf16[10,128,128]{2,1,0:T(8,128)(2,1)}, u32[]{:S(2)}, u32[]{:S(2)}) collective-permute-start(bf16[10,128,128]{2,1,0:T(8,128)(2,1)} %pack.3), channel_id=1, source_target_pairs={{0,48},{8,56},{16,0},{24,8},{32,16},{40,24},{48,32},{56,40},{64,11... | collective-permute-start | bytes 983048 | tf_op jit(solution)/shard_map/ppermute | solution.py:42
  44.2 20.2 %collective-permute-start.11 = (bf16[10,128,128]{2,1,0:T(8,128)(2,1)}, bf16[10,128,128]{2,1,0:T(8,128)(2,1)}, u32[]{:S(2)}, u32[]{:S(2)}) collective-permute-start(bf16[10,128,128]{2,1,0:T(8,128)(2,1)} %pack.3), channel_id=1, source_target_pairs={{0,16},{8,24},{16,32},{24,40},{32,48},{40,56},{48,0},{56,8},{64,80... | collective-permute-start | bytes 983048 | tf_op jit(solution)/shard_map/ppermute | solution.py:42
  50.5 41.0 %collective-permute-start.9 = (bf16[256,2048]{1,0:T(8,128)(2,1)}, bf16[256,2048]{1,0:T(8,128)(2,1)}, u32[]{:S(2)}, u32[]{:S(2)}) collective-permute-start(bf16[256,2048]{1,0:T(8,128)(2,1)} %get-tuple-element.19), channel_id=1, source_target_pairs={{0,8},{8,16},{16,24},{24,32},{32,40},{40,48},{48,56},{56,64},{64,7... | collective-permute-start | bytes 3145736 | tf_op jit(solution)/shard_map/ppermute | solution.py:396
  65.4 16.7 %collective-permute-start.14 = (bf16[2,10,128,128]{3,2,1,0:T(8,128)(2,1)S(1)}, bf16[2,10,128,128]{3,2,1,0:T(8,128)(2,1)S(1)}, u32[]{:S(2)}, u32[]{:S(2)}) collective-permute-start(bf16[2,10,128,128]{3,2,1,0:T(8,128)(2,1)S(1)} %pad_maximum_fusion.rest_1_.rest_0_.refs_4_), channel_id=1, source_target_pairs={{0,64},{8,72},{16,80},{24,88},{32,96},{40,104},{48,112},{56,120},{... | collective-permute-start | bytes 1966088 | tf_op jit(solution)/shard_map/ppermute | solution.py:42
  66.7 23.5 %collective-permute-start.15 = (bf16[2,10,128,128]{3,2,1,0:T(8,128)(2,1)S(1)}, bf16[2,10,128,128]{3,2,1,0:T(8,128)(2,1)S(1)}, u32[]{:S(2)}, u32[]{:S(2)}) collective-permute-start(bf16[2,10,128,128]{3,2,1,0:T(8,128)(2,1)S(1)} %pad_maximum_fusion.1.rest_2_.rest_1_.refs_5_), channel_id=1, source_target_pairs={{0,65},{8,73},{16,81},{24,89},{32,97},{40,105},{48,113},{56,121},{... | collective-permute-start | bytes 1966088 | tf_op jit(solution)/shard_map/ppermute | solution.py:42
  68.1 39.8 %collective-permute-start.16 = (bf16[2,10,128,128]{3,2,1,0:T(8,128)(2,1)S(1)}, bf16[2,10,128,128]{3,2,1,0:T(8,128)(2,1)S(1)}, u32[]{:S(2)}, u32[]{:S(2)}) collective-permute-start(bf16[2,10,128,128]{3,2,1,0:T(8,128)(2,1)S(1)} %pad_maximum_fusion.rest_1_.rest_0_.refs_4_), channel_id=1, source_target_pairs={{0,8},{8,0},{16,24},{24,16},{32,40},{40,32},{48,56},{56,48},{64,72... | collective-permute-start | bytes 1966088 | tf_op jit(solution)/shard_map/ppermute | solution.py:42
  68.1 40.6 %collective-permute-start.17 = (bf16[2,10,128,128]{3,2,1,0:T(8,128)(2,1)S(1)}, bf16[2,10,128,128]{3,2,1,0:T(8,128)(2,1)}, u32[]{:S(2)}, u32[]{:S(2)}) collective-permute-start(bf16[2,10,128,128]{3,2,1,0:T(8,128)(2,1)S(1)} %pad_maximum_fusion.1.rest_2_.rest_1_.refs_5_), channel_id=1, source_target_pairs={{0,8},{8,0},{16,24},{24,16},{32,40},{40,32},{48,56},{56,48},{64,72... | collective-permute-start | bytes 1966088 | tf_op jit(solution)/shard_map/ppermute | solution.py:42
  82.1 27.7 %collective-permute-start.18 = (bf16[2,10,128,128]{3,2,1,0:T(8,128)(2,1)S(1)}, bf16[2,10,128,128]{3,2,1,0:T(8,128)(2,1)}, u32[]{:S(2)}, u32[]{:S(2)}) collective-permute-start(bf16[2,10,128,128]{3,2,1,0:T(8,128)(2,1)S(1)} %collective-permute-done.14.rest_3_.rest_2_.refs_6_), channel_id=1, source_target_pairs={{0,8},{8,0},{16,24},{24,16},{32,40},{40,32},{48,56},{56,48},{64,72... | collective-permute-start | bytes 1966088 | tf_op jit(solution)/shard_map/ppermute | solution.py:42
  90.2 19.6 %collective-permute-start.19 = (bf16[2,10,128,128]{3,2,1,0:T(8,128)(2,1)S(1)}, bf16[2,10,128,128]{3,2,1,0:T(8,128)(2,1)}, u32[]{:S(2)}, u32[]{:S(2)}) collective-permute-start(bf16[2,10,128,128]{3,2,1,0:T(8,128)(2,1)S(1)} %collective-permute-done.15.rest_4_.rest_3_.refs_7_), channel_id=1, source_target_pairs={{0,8},{8,0},{16,24},{24,16},{32,40},{40,32},{48,56},{56,48},{64,72... | collective-permute-start | bytes 1966088 | tf_op jit(solution)/shard_map/ppermute | solution.py:42
  105.9 20.9 %collective-permute-start.26 = (bf16[1024,256]{1,0:T(8,128)(2,1)}, bf16[1024,256]{1,0:T(8,128)(2,1)S(1)}, u32[]{:S(2)}, u32[]{:S(2)}) collective-permute-start(bf16[1024,256]{1,0:T(8,128)(2,1)} %attend.5.refs_0_), channel_id=1, source_target_pairs={{0,2},{2,4},{4,6},{6,0},{1,3},{3,5},{5,7},{7,1},{8,10},{10,12},{12... | collective-permute-start | bytes 1572872 | tf_op jit(solution)/shard_map/ppermute | solution.py:400
  107.9 27.7 %collective-permute-start.27 = (bf16[1024,256]{1,0:T(8,128)(2,1)}, bf16[1024,256]{1,0:T(8,128)(2,1)S(1)}, u32[]{:S(2)}, u32[]{:S(2)}) collective-permute-start(bf16[1024,256]{1,0:T(8,128)(2,1)} %attend.5.refs_0_), channel_id=1, source_target_pairs={{0,6},{2,0},{4,2},{6,4},{1,7},{3,1},{5,3},{7,5},{8,14},{10,8},{12,... | collective-permute-start | bytes 1572872 | tf_op jit(solution)/shard_map/ppermute | solution.py:400
  108.7 28.5 %collective-permute-start.28 = (bf16[1024,256]{1,0:T(8,128)(2,1)}, bf16[1024,256]{1,0:T(8,128)(2,1)S(1)}, u32[]{:S(2)}, u32[]{:S(2)}) collective-permute-start(bf16[1024,256]{1,0:T(8,128)(2,1)} %attend.5.refs_0_), channel_id=1, source_target_pairs={{0,4},{2,6},{4,0},{6,2},{1,5},{3,7},{5,1},{7,3},{8,12},{10,14},{12... | collective-permute-start | bytes 1572872 | tf_op jit(solution)/shard_map/ppermute | solution.py:400
  124.1 36.7 %collective-permute-start.20 = (bf16[768,256]{1,0:T(8,128)(2,1)}, bf16[768,256]{1,0:T(8,128)(2,1)S(1)}, u32[]{:S(2)}, u32[]{:S(2)}) collective-permute-start(bf16[768,256]{1,0:T(8,128)(2,1)} %attend.6.refs_0_), channel_id=1, source_target_pairs={{0,2},{2,4},{4,6},{6,0},{1,3},{3,5},{5,7},{7,1},{8,10},{10,12},{12... | collective-permute-start | bytes 1179656 | tf_op jit(solution)/shard_map/ppermute | solution.py:400
  124.2 36.6 %collective-permute-start.21 = (bf16[768,256]{1,0:T(8,128)(2,1)}, bf16[768,256]{1,0:T(8,128)(2,1)S(1)}, u32[]{:S(2)}, u32[]{:S(2)}) collective-permute-start(bf16[768,256]{1,0:T(8,128)(2,1)} %attend.6.refs_0_), channel_id=1, source_target_pairs={{0,6},{2,0},{4,2},{6,4},{1,7},{3,1},{5,3},{7,5},{8,14},{10,8},{12,... | collective-permute-start | bytes 1179656 | tf_op jit(solution)/shard_map/ppermute | solution.py:400
  126.9 34.0 %collective-permute-start.22 = (bf16[768,256]{1,0:T(8,128)(2,1)}, bf16[768,256]{1,0:T(8,128)(2,1)S(1)}, u32[]{:S(2)}, u32[]{:S(2)}) collective-permute-start(bf16[768,256]{1,0:T(8,128)(2,1)} %attend.6.refs_0_), channel_id=1, source_target_pairs={{0,4},{2,6},{4,0},{6,2},{1,5},{3,7},{5,1},{7,3},{8,12},{10,14},{12... | collective-permute-start | bytes 1179656 | tf_op jit(solution)/shard_map/ppermute | solution.py:400
  136.4 15.4 %collective-permute-start.23 = (bf16[256,256]{1,0:T(8,128)(2,1)}, bf16[256,256]{1,0:T(8,128)(2,1)S(1)}, u32[]{:S(2)}, u32[]{:S(2)}) collective-permute-start(bf16[256,256]{1,0:T(8,128)(2,1)} %attend.7.refs_4_), channel_id=1, source_target_pairs={{0,2},{2,4},{4,6},{6,0},{1,3},{3,5},{5,7},{7,1},{8,10},{10,12},{12... | collective-permute-start | bytes 393224 | tf_op jit(solution)/shard_map/ppermute | solution.py:400
  137.1 23.6 %collective-permute-start.24 = (bf16[256,256]{1,0:T(8,128)(2,1)}, bf16[256,256]{1,0:T(8,128)(2,1)S(1)}, u32[]{:S(2)}, u32[]{:S(2)}) collective-permute-start(bf16[256,256]{1,0:T(8,128)(2,1)} %attend.7.refs_4_), channel_id=1, source_target_pairs={{0,6},{2,0},{4,2},{6,4},{1,7},{3,1},{5,3},{7,5},{8,14},{10,8},{12,... | collective-permute-start | bytes 393224 | tf_op jit(solution)/shard_map/ppermute | solution.py:400
  (29 other events, 365.0 us)

commit v2 on v1

--- a/solution.py
+++ b/solution.py
@@ -11,10 +11,11 @@
 HEAD_DIM = 128
 X_LO, Z, CORE, X = 2, 4, 2, 4
 CHUNK_HEADS = (2, 2)
-RUNS = ((12, 4), (0, 12))
+RUNS = ((8, 8), (0, 8))
 GROUP = 4
-LAG = 1
-AHEAD = 1
+LAG = 2
+AHEAD = 0
+STAGES = {0: (0,), 1: (1, 2, 3)}
 
 
 def route(move):
@@ -122,14 +123,20 @@
     )(*weights, *tail)
 
 
-def origins(me):
+def origins():
+    me = lax.axis_index("seq")
     x_lo, z, c = me // (Z * CORE), (me // CORE) % Z, me % CORE
-    found = []
-    for core in (c, 1 - c):
-        for x in (x_lo, 1 - x_lo):
-            for dz in (0, 3, 1, 2):
-                found.append((x * Z + (z + dz) % Z) * CORE + core)
-    return jnp.stack(found).astype(jnp.int32)
+    return [
+        (x * Z + (z + dz) % Z) * CORE + core
+        for core in (c, 1 - c)
+        for x in (x_lo, 1 - x_lo)
+        for dz in (0, 3, 1, 2)
+    ]
+
+
+def head_origins():
+    me = lax.axis_index("head")
+    return [(me + d) % 4 for d in (0, 3, 1, 2)]
 
 
 def only_head(q, h, heads):
@@ -139,9 +146,9 @@
     )
 
 
-def attend_kernel(heads, first, group, skip, slots, rows, bank, normed, *rest):
+def attend_kernel(heads, first, group, slots, bank, normed, *rest):
     arrived, rest = (rest[0], rest[1:]) if first == 0 else (None, rest)
-    pieces, out, ctx, w, x, ctx_sem, w_sem, x_sem = rest[:8], *rest[8 + skip :]
+    pieces, out, ctx, w, x, ctx_sem, w_sem, x_sem = rest[:8], *rest[8:]
     step, steps = pl.program_id(0), pl.num_programs(0)
     width = heads * HEAD_DIM
     kv_rows = bank.shape[1]
@@ -178,6 +185,7 @@
 
     @pl.when(step == 0)
     def _():
+        rows = origins()
         for i in range(8):
             for k in range(2):
                 at = pl.multiple_of(rows[i * 2 + k] * shard, shard)
@@ -207,10 +215,10 @@
         kv, weights = {}, {}
         for j in range(group + 2 * LAG):
             if j < group:
-                if starting:
-                    pltpu.make_async_copy(blocks[j], blocks[j], ctx_sem.at[slot, j]).wait()
-                    if j == AHEAD:
-                        fetch_next()
+                for k in STAGES.get(j, ()) if starting else ():
+                    pltpu.make_async_copy(blocks[k], blocks[k], ctx_sem.at[slot, k]).wait()
+                if starting and j == AHEAD:
+                    fetch_next()
                 kv[j] = jnp.dot(blocks[j][...], wkv, preferred_element_type=jnp.float32).astype(jnp.bfloat16)
             i = j - LAG
             if 0 <= i < group:
@@ -238,24 +246,22 @@
         compute(False)
 
 
-def attend(slots, rows, bank, arrived, normed, pieces, heads, first, blocks, group, whole=False, into=None):
+def attend(slots, bank, arrived, normed, pieces, heads, first, blocks, group):
     model = normed.shape[1]
     kv_rows = bank.shape[1]
     arrived = [arrived] if first == 0 else []
-    into = [] if into is None else [into]
-    at = first // group if whole else 0
     block = normed.shape[0] // bank.shape[0]
     width = heads * HEAD_DIM
     hbm = pl.BlockSpec(memory_space=pltpu.HBM)
     flops = 2 * blocks * (2 * kv_rows + block) * model * width
     return pl.pallas_call(
-        functools.partial(attend_kernel, heads, first, group, len(into)),
-        out_shape=jax.ShapeDtypeStruct((normed.shape[0] if whole else blocks * block, width), jnp.bfloat16),
+        functools.partial(attend_kernel, heads, first, group),
+        out_shape=jax.ShapeDtypeStruct((blocks * block, width), jnp.bfloat16),
         grid_spec=pltpu.PrefetchScalarGridSpec(
-            num_scalar_prefetch=2,
+            num_scalar_prefetch=1,
             grid=(blocks // group,),
-            in_specs=[hbm] * (2 + len(arrived) + 8 + len(into)),
-            out_specs=pl.BlockSpec((group * block, width), lambda i, *_: (at + i, 0)),
+            in_specs=[hbm] * (2 + len(arrived) + 8),
+            out_specs=pl.BlockSpec((group * block, width), lambda i, *_: (i, 0)),
             scratch_shapes=[
                 pltpu.VMEM((2, group * kv_rows, model), jnp.bfloat16),
                 pltpu.VMEM((3 * heads, model, HEAD_DIM), jnp.bfloat16),
@@ -265,122 +271,122 @@
                 pltpu.SemaphoreType.DMA((2,)),
             ],
         ),
-        input_output_aliases={4 + len(arrived) + 8: 0} if into else {},
         cost_estimate=pl.CostEstimate(
             flops=flops, bytes_accessed=2 * blocks * kv_rows * model, transcendentals=0
         ),
         compiler_params=pltpu.CompilerParams(vmem_limit_bytes=60 * 2**20),
         name="attend",
-    )(slots, rows, bank, normed, *arrived, *pieces, *into)
-
-
-def load_parts(parts, cols, att, start, sem):
-    tall, width = parts[0].shape
-    for k in range(4):
-        c = pl.multiple_of(cols[k] * width, width)
-        pltpu.make_async_copy(parts[k], att.at[pl.ds(start, tall), pl.ds(c, width)], sem).start()
-
-
-def project_first_kernel(rows, cols, *refs):
-    parts, pieces = refs[:4], refs[4:12]
-    out, w_next, w, att, att_sem, w_sem, next_sem = refs[12:]
+    )(slots, bank, normed, *arrived, *pieces)
+
+
+def load_parts(parts, att, sem):
+    width = parts[0].shape[1]
+    for part, origin in zip(parts, head_origins()):
+        pltpu.make_async_copy(part, att.at[:, pl.ds(pl.multiple_of(origin * width, width), width)], sem).start()
+
+
+def project_first_kernel(*refs):
+    parts, pieces = refs[:12], refs[12:20]
+    out, share, w_next, w, att, att_sem, w_sem, next_sem = refs[20:]
     deep, wide = w.shape[0] // 4, w.shape[1] // 4
     tile = pieces[0].shape[2]
     count = deep // tile
     lead = pieces[0].shape[1] - 2 * count
-    load_parts(parts, cols, att, 0, att_sem)
+    rows = origins()
+    for i in range(2):
+        load_parts(parts[4 * i : 4 * i + 4], att.at[i], att_sem.at[i])
     for dst, sem, at in ((w, w_sem, lead), (w_next, next_sem, lead + count)):
         for i in range(8):
             for k in range(2):
-                origin = rows[i * 2 + k]
-                r = pl.multiple_of((origin // 4) * deep, deep)
-                c = pl.multiple_of((origin % 4) * wide, wide)
+                r = pl.multiple_of((rows[i * 2 + k] // 4) * deep, deep)
+                c = pl.multiple_of((rows[i * 2 + k] % 4) * wide, wide)
                 for t in range(count):
                     pltpu.make_async_copy(
                         pieces[i].at[k, at + t], dst.at[pl.ds(r + t * tile, tile), pl.ds(c, wide)], sem
                     ).start()
-    pltpu.make_async_copy(att, att, att_sem).wait()
+    load_parts(parts[8:], att.at[2], att_sem.at[2])
+    for i in range(2):
+        pltpu.make_async_copy(att.at[i], att.at[i], att_sem.at[i]).wait()
     pltpu.make_async_copy(w, w, w_sem).wait()
-    out[...] = jnp.dot(att[...], w[...], preferred_element_type=jnp.float32)
+    share[...] = jnp.dot(att[1], w[...], preferred_element_type=jnp.float32)
+    begun = jnp.dot(att[0], w[...], preferred_element_type=jnp.float32)
     pltpu.make_async_copy(w_next, w_next, next_sem).wait()
-
-
-def project_first(rows, cols, parts, pieces, wide):
-    tall, deep = parts[0].shape[0], 4 * parts[0].shape[1]
+    pltpu.make_async_copy(att.at[2], att.at[2], att_sem.at[2]).wait()
+    rest = jnp.dot(att[2], w_next[...], preferred_element_type=jnp.float32)
+    out[...] = (begun + rest).astype(jnp.bfloat16)
+
+
+def project_first(early, late, first, second, pieces, tall, wide):
+    rows, width = first[early][0].shape
+    deep = 4 * width
     hbm = pl.BlockSpec(memory_space=pltpu.HBM)
+    parts = [*first[early], *first[late], *second[early]]
+    at = early[0] // early[1]
     return pl.pallas_call(
         project_first_kernel,
-        out_shape=(jax.ShapeDtypeStruct((tall, wide), jnp.float32), jax.ShapeDtypeStruct((deep, wide), jnp.bfloat16)),
-        grid_spec=pltpu.PrefetchScalarGridSpec(
-            num_scalar_prefetch=2,
-            grid=(1,),
-            in_specs=[hbm] * 12,
-            out_specs=(
-                pl.BlockSpec((tall, wide), lambda i, *_: (0, 0)),
-                pl.BlockSpec((deep, wide), lambda i, *_: (0, 0)),
-            ),
-            scratch_shapes=[
-                pltpu.VMEM((deep, wide), jnp.bfloat16),
-                pltpu.VMEM((tall, deep), jnp.bfloat16),
-                pltpu.SemaphoreType.DMA,
-                pltpu.SemaphoreType.DMA,
-                pltpu.SemaphoreType.DMA,
-            ],
-        ),
+        out_shape=(
+            jax.ShapeDtypeStruct((tall, wide), jnp.bfloat16),
+            jax.ShapeDtypeStruct((rows, wide), jnp.float32),
+            jax.ShapeDtypeStruct((deep, wide), jnp.bfloat16),
+        ),
+        grid=(1,),
+        in_specs=[hbm] * (len(parts) + 8),
+        out_specs=(
+            pl.BlockSpec((rows, wide), lambda i: (at, 0)),
+            pl.BlockSpec((rows, wide), lambda i: (0, 0)),
+            pl.BlockSpec((deep, wide), lambda i: (0, 0)),
+        ),
+        scratch_shapes=[
+            pltpu.VMEM((deep, wide), jnp.bfloat16),
+            pltpu.VMEM((3, rows, deep), jnp.bfloat16),
+            pltpu.SemaphoreType.DMA((3,)),
+            pltpu.SemaphoreType.DMA,
+            pltpu.SemaphoreType.DMA,
+        ],
         compiler_params=pltpu.CompilerParams(vmem_limit_bytes=60 * 2**20),
         cost_estimate=pl.CostEstimate(flops=2 * tall * deep * wide, bytes_accessed=2**23, transcendentals=0),
         name="project_first",
-    )(rows, cols, *parts, *pieces)
-
-
-def project_last_kernel(starts, cols, *refs):
-    n = 4 * len(starts)
-    parts, (w_in, share_in, out, w, share, att, w_sem, sem, att_sem) = refs[:n], refs[n:]
+    )(*parts, *pieces)
+
+
+def project_last_kernel(*refs):
+    parts, (w_in, share_in, _, out, w, share, att, w_sem, sem, att_sem) = refs[:4], refs[4:]
+    load_parts(parts, att, att_sem)
     pltpu.make_async_copy(w_in, w, w_sem).start()
-    for i, start in enumerate(starts):
-        load_parts(parts[4 * i : 4 * i + 4], cols, att, start, att_sem)
     pltpu.make_async_copy(share_in, share, sem).start()
+    pltpu.make_async_copy(att, att, att_sem).wait()
     pltpu.make_async_copy(w, w, w_sem).wait()
-    pltpu.make_async_copy(att, att, att_sem).wait()
     pltpu.make_async_copy(share, share, sem).wait()
     rest = jnp.dot(att[...], w[...], preferred_element_type=jnp.float32)
     out[...] = (share[...] + rest).astype(jnp.bfloat16)
 
 
-def project_last(cols, runs, weights, share):
-    (tall, wide), deep = share.shape, weights.shape[0]
+def project_last(late, parts, weights, share, out):
+    (rows, wide), deep = share.shape, weights.shape[0]
     hbm = pl.BlockSpec(memory_space=pltpu.HBM)
-    starts = tuple(start for start, _ in runs)
-    parts = [p for _, four in runs for p in four]
+    at = late[0] // late[1]
     return pl.pallas_call(
-        functools.partial(project_last_kernel, starts),
-        out_shape=jax.ShapeDtypeStruct((tall, wide), jnp.bfloat16),
-        grid_spec=pltpu.PrefetchScalarGridSpec(
-            num_scalar_prefetch=1,
-            grid=(1,),
-            in_specs=[hbm] * (len(parts) + 2),
-            out_specs=pl.BlockSpec((tall, wide), lambda i, *_: (0, 0)),
-            scratch_shapes=[
-                pltpu.VMEM((deep, wide), jnp.bfloat16),
-                pltpu.VMEM((tall, wide), jnp.float32),
-                pltpu.VMEM((tall, deep), jnp.bfloat16),
-                pltpu.SemaphoreType.DMA,
-                pltpu.SemaphoreType.DMA,
-                pltpu.SemaphoreType.DMA,
-            ],
-        ),
+        project_last_kernel,
+        out_shape=jax.ShapeDtypeStruct(out.shape, out.dtype),
+        grid=(1,),
+        in_specs=[hbm] * 7,
+        out_specs=pl.BlockSpec((rows, wide), lambda i: (at, 0)),
+        scratch_shapes=[
+            pltpu.VMEM((deep, wide), jnp.bfloat16),
+            pltpu.VMEM((rows, wide), jnp.float32),
+            pltpu.VMEM((rows, deep), jnp.bfloat16),
+            pltpu.SemaphoreType.DMA,
+            pltpu.SemaphoreType.DMA,
+            pltpu.SemaphoreType.DMA,
+        ],
+        input_output_aliases={6: 0},
         compiler_params=pltpu.CompilerParams(vmem_limit_bytes=60 * 2**20),
-        cost_estimate=pl.CostEstimate(flops=2 * tall * deep * wide, bytes_accessed=2**23, transcendentals=0),
+        cost_estimate=pl.CostEstimate(flops=2 * rows * deep * wide, bytes_accessed=2**22, transcendentals=0),
         name="project_last",
-    )(cols, *parts, weights, share)
+    )(*parts, weights, share, out)
 
 
 def local(tokens, neighbor_bank, slots, w_query, w_key, w_value, w_out):
-    blocks = neighbor_bank.shape[0]
-    me, head_at = lax.axis_index("seq"), lax.axis_index("head")
-    rows = origins(me)
-    cols = jnp.stack([(head_at + d) % 4 for d in (0, 3, 1, 2)]).astype(jnp.int32)
-
     swap = [
         ((4 * a + j) * 4 + b, (4 * b + j) * 4 + a) for a in range(4) for b in range(4) for j in range(4)
     ]
@@ -396,28 +402,27 @@
     arrived = lax.ppermute(last, "seq", [(i, i + 1) for i in range(devices - 1)])
     pieces = gather_core(x_first)
 
-    block = tokens.shape[0] // blocks
     ring = lambda block, d: lax.ppermute(block, "head", [(i, (i + d) % 4) for i in range(4)])
 
     def exchange(own):
         return [own, ring(own, 1), ring(own, -1), ring(own, 2)]
 
-    heads, x, own = CHUNK_HEADS[0], normed, None
-    for n, (start, count) in enumerate(RUNS):
-        own = attend(slots, rows, neighbor_bank, arrived, x, pieces, heads, start, count, GROUP, whole=True, into=own)
-        x = after(normed, own)
-        if n == 0:
-            x_second = gather_x([after(p, own) for p in z_second])
-    pieces = gather_core(x_second)
-    first_parts = exchange(own)
-
-    heads, runs = CHUNK_HEADS[1], []
-    for n, (start, count) in enumerate(RUNS[::-1], 2):
-        own = attend(slots, rows, neighbor_bank, arrived, x, pieces, heads, start, count, GROUP)
-        x = after(normed, own)
-        runs.append((start * block, exchange(own)))
-    share, weights = project_first(rows, cols, first_parts, pieces, w_out.shape[0])
-    return project_last(cols, runs, weights, share)
+    x, chunks, n = normed, [], 0
+    for heads, order in zip(CHUNK_HEADS, (RUNS, RUNS[::-1])):
+        runs = {}
+        for start, count in order:
+            own = attend(slots, neighbor_bank, arrived, x, pieces, heads, start, count, GROUP)
+            x = after(normed, own)
+            runs[start, count] = exchange(own)
+            if n == 0:
+                x_second = gather_x([after(p, own) for p in z_second])
+            if n == 1:
+                pieces = gather_core(x_second)
+            n += 1
+        chunks.append(runs)
+    late, early = RUNS
+    out, share, weights = project_first(early, late, *chunks, pieces, tokens.shape[0], w_out.shape[0])
+    return project_last(late, chunks[1][late], weights, share, out)
 
 
 def solution(mesh):

time: 169 us -> 160 us (0.947)
  the two profiles are of different devices: /device:TPU:3 before, /device:TPU:1 now
where the time goes in v2:
time: 160 us
  Pallas kernels  62.4 us (39%)
  starting transfers between devices  56 us (35%)
  waiting for transfers between devices  36.4 us (23%)
  local copies, waits for them, and re-layouts  2.26 us (1%)
  other arithmetic  2.1 us (1%)
    pallas_call x4, Pallas kernels, attend(): pl.pallas_call(functools.partial(attend_kernel, heads, first, group), out...  45.4 us
    ppermute x18, starting transfers between devices, plane(): return lax.ppermute(block, ('seq', 'batch'), pairs)  32.4 us
    ppermute x18, waiting for transfers between devices, plane(): return lax.ppermute(block, ('seq', 'batch'), pairs)  28.8 us
    ppermute x12, starting transfers between devices, local(): lax.ppermute(block, 'head', [(i, (i + d) % 4) for i in range(4)])  18.6 us
    ppermute x12, waiting for transfers between devices, local(): lax.ppermute(block, 'head', [(i, (i + d) % 4) for i in range(4)])  7.55 us
    pallas_call x1, Pallas kernels, prepare(): pl.pallas_call(prepare_kernel, out_shape=(jax.ShapeDtypeStruct(tokens.sha...  5.32 us
    pallas_call x1, Pallas kernels, project_first(): pl.pallas_call(project_first_kernel, out_shape=(jax.ShapeDtypeStruct((tal...  5.22 us
    ppermute x1, starting transfers between devices, local(): lax.ppermute(last, 'seq', [(i, i + 1) for i in range(devices - 1)])  3.43 us
  transfers between devices with their start and end apart: 32, of which 10 were waited for; matrix products, arithmetic and copies ran while one was open for 1% of the time, Pallas kernels for 36%

profile of v2, /device:TPU:1, one launch (start us, length us, event | category | flops | bytes accessed | tf_op | source)
XLA Modules:
  0.0 159.8 jit_solution(10369242218309477402)
XLA Ops:
  1.5 2.5 %collective-permute-start = (bf16[6,128,128]{2,1,0:T(8,128)(2,1)}, bf16[6,128,128]{2,1,0:T(8,128)(2,1)S(1)}, u32[]{:S(2)}, u32[]{:S(2)}) collective-permute-start(bf16[6,128,128]{2,1,0:T(8,128)(2,1)} %pack.2), channel_id=1, source_target_pairs={{0,16},{8,24},{16,32},{24,40},{32,48},{40,56},{48,0},{56,8},{64,80... | collective-permute-start | bytes 589832 | tf_op jit(solution)/shard_map/ppermute | solution.py:43
  4.1 3.3 %collective-permute-start.2 = (bf16[6,128,128]{2,1,0:T(8,128)(2,1)}, bf16[6,128,128]{2,1,0:T(8,128)(2,1)S(1)}, u32[]{:S(2)}, u32[]{:S(2)}) collective-permute-start(bf16[6,128,128]{2,1,0:T(8,128)(2,1)} %pack.2), channel_id=1, source_target_pairs={{0,32},{8,40},{16,48},{24,56},{32,0},{40,8},{48,16},{56,24},{64,96... | collective-permute-start | bytes 589832 | tf_op jit(solution)/shard_map/ppermute | solution.py:43
  8.1 2.9 %collective-permute-done = bf16[6,128,128]{2,1,0:T(8,128)(2,1)S(1)} collective-permute-done((bf16[6,128,128]{2,1,0:T(8,128)(2,1)}, bf16[6,128,128]{2,1,0:T(8,128)(2,1)S(1)}, u32[]{:S(2)}, u32[]{:S(2)}) %collective-permute-start) | collective-permute-done | bytes 196640 | tf_op jit(solution)/shard_map/ppermute | solution.py:43
  13.2 2.9 %collective-permute-done.2 = bf16[6,128,128]{2,1,0:T(8,128)(2,1)S(1)} collective-permute-done((bf16[6,128,128]{2,1,0:T(8,128)(2,1)}, bf16[6,128,128]{2,1,0:T(8,128)(2,1)S(1)}, u32[]{:S(2)}, u32[]{:S(2)}) %collective-permute-start.2) | collective-permute-done | bytes 196640 | tf_op jit(solution)/shard_map/ppermute | solution.py:43
  16.2 2.5 %collective-permute-start.4 = (bf16[2,6,128,128]{3,2,1,0:T(8,128)(2,1)S(1)}, bf16[2,6,128,128]{3,2,1,0:T(8,128)(2,1)S(1)}, u32[]{:S(2)}, u32[]{:S(2)}) collective-permute-start(bf16[2,6,128,128]{3,2,1,0:T(8,128)(2,1)S(1)} %pad_maximum_fusion.3.rest_1_.rest_2_), channel_id=1, source_target_pairs={{0,65},{8,73},{16,81},{24,89},{32,97},{40,105},{48,113},{56,121},{... | collective-permute-start | bytes 1179656 | tf_op jit(solution)/shard_map/ppermute | solution.py:43
  25.7 2.4 %collective-permute-start.8 = (bf16[2,6,128,128]{3,2,1,0:T(8,128)(2,1)S(1)}, bf16[2,6,128,128]{3,2,1,0:T(8,128)(2,1)S(1)}, u32[]{:S(2)}, u32[]{:S(2)}) collective-permute-start(bf16[2,6,128,128]{3,2,1,0:T(8,128)(2,1)S(1)} %collective-permute-done.4.rest_3_.rest_4_), channel_id=1, source_target_pairs={{0,8},{8,0},{16,24},{24,16},{32,40},{40,32},{48,56},{56,48},{64,72... | collective-permute-start | bytes 1179656 | tf_op jit(solution)/shard_map/ppermute | solution.py:43
  29.6 5.3 %prepare.1 = (bf16[1024,2048]{1,0:T(8,128)(2,1)}, bf16[256,2048]{1,0:T(8,128)(2,1)}) custom-call(s32[16]{0:T(128)} %slots.9, bf16[16,256,2048]{2,1,0:T(8,128)(2,1)} %bank.9, bf16[1024,2048]{1,0:T(8,128)(2,1)} %tokens.1), custom_call_target="tpu_custom_call" | custom-call | flops 1073741824 | bytes 8388608 | tf_op jit(solution)/shard_map/prepare/pallas_call | solution.py:83
  35.0 3.4 %collective-permute-start.9 = (bf16[256,2048]{1,0:T(8,128)(2,1)}, bf16[256,2048]{1,0:T(8,128)(2,1)}, u32[]{:S(2)}, u32[]{:S(2)}) collective-permute-start(bf16[256,2048]{1,0:T(8,128)(2,1)} %get-tuple-element.20), channel_id=1, source_target_pairs={{0,8},{8,16},{16,24},{24,32},{32,40},{40,48},{48,56},{56,64},{64,7... | collective-permute-start | bytes 3145736 | tf_op jit(solution)/shard_map/ppermute | solution.py:402
  40.1 3.3 %collective-permute-start.11 = (bf16[10,128,128]{2,1,0:T(8,128)(2,1)}, bf16[10,128,128]{2,1,0:T(8,128)(2,1)S(1)}, u32[]{:S(2)}, u32[]{:S(2)}) collective-permute-start(bf16[10,128,128]{2,1,0:T(8,128)(2,1)} %pack.3), channel_id=1, source_target_pairs={{0,16},{8,24},{16,32},{24,40},{32,48},{40,56},{48,0},{56,8},{64,80... | collective-permute-start | bytes 983048 | tf_op jit(solution)/shard_map/ppermute | solution.py:43
  43.4 4.6 %collective-permute-start.13 = (bf16[10,128,128]{2,1,0:T(8,128)(2,1)}, bf16[10,128,128]{2,1,0:T(8,128)(2,1)S(1)}, u32[]{:S(2)}, u32[]{:S(2)}) collective-permute-start(bf16[10,128,128]{2,1,0:T(8,128)(2,1)} %pack.3), channel_id=1, source_target_pairs={{0,32},{8,40},{16,48},{24,56},{32,0},{40,8},{48,16},{56,24},{64,96... | collective-permute-start | bytes 983048 | tf_op jit(solution)/shard_map/ppermute | solution.py:43
  49.0 11.0 %attend.4.refs_4_ = bf16[512,256]{1,0:T(8,128)(2,1)} custom-call(s32[16]{0:T(128)} %slots.9, bf16[16,256,2048]{2,1,0:T(8,128)(2,1)} %bank.9, bf16[1024,2048]{1,0:T(8,128)(2,1)} %get-tuple-element.27.normed, bf16[2,6,128,128]{3,2,1,0:T(8,128)(2,1)} %copy-done.6, bf16[2,6,128,128]{3,2,1,0:T(8,128)(2,1)} %copy-done.7, bf16[2,6,128,128]{3,2,1,0:T(8,128)(2,1)} %copy-done.8, ...), custom_call_target="tpu_custom_call" | custom-call | flops 4831838208 | bytes 8388608 | tf_op jit(solution)/shard_map/attend/pallas_call | solution.py:257
  61.1 9.7 %collective-permute-done.13 = bf16[10,128,128]{2,1,0:T(8,128)(2,1)S(1)} collective-permute-done((bf16[10,128,128]{2,1,0:T(8,128)(2,1)}, bf16[10,128,128]{2,1,0:T(8,128)(2,1)S(1)}, u32[]{:S(2)}, u32[]{:S(2)}) %collective-permute-start.13) | collective-permute-done | bytes 327712 | tf_op jit(solution)/shard_map/ppermute | solution.py:43
  70.8 4.6 %collective-permute-start.14 = (bf16[2,10,128,128]{3,2,1,0:T(8,128)(2,1)S(1)}, bf16[2,10,128,128]{3,2,1,0:T(8,128)(2,1)S(1)}, u32[]{:S(2)}, u32[]{:S(2)}) collective-permute-start(bf16[2,10,128,128]{3,2,1,0:T(8,128)(2,1)S(1)} %pad_maximum_fusion.rest_1_.rest_0_.refs_12_), channel_id=1, source_target_pairs={{0,64},{8,72},{16,80},{24,88},{32,96},{40,104},{48,112},{56,120},{... | collective-permute-start | bytes 1966088 | tf_op jit(solution)/shard_map/ppermute | solution.py:43
  76.4 2.6 %collective-permute-start.15 = (bf16[2,10,128,128]{3,2,1,0:T(8,128)(2,1)S(1)}, bf16[2,10,128,128]{3,2,1,0:T(8,128)(2,1)S(1)}, u32[]{:S(2)}, u32[]{:S(2)}) collective-permute-start(bf16[2,10,128,128]{3,2,1,0:T(8,128)(2,1)S(1)} %pad_maximum_fusion.1.rest_2_.rest_1_.refs_13_), channel_id=1, source_target_pairs={{0,65},{8,73},{16,81},{24,89},{32,97},{40,105},{48,113},{56,121},{... | collective-permute-start | bytes 1966088 | tf_op jit(solution)/shard_map/ppermute | solution.py:43
  79.4 8.2 %collective-permute-done.14.rest_3_.rest_2_.refs_14_ = bf16[2,10,128,128]{3,2,1,0:T(8,128)(2,1)S(1)} collective-permute-done((bf16[2,10,128,128]{3,2,1,0:T(8,128)(2,1)S(1)}, bf16[2,10,128,128]{3,2,1,0:T(8,128)(2,1)S(1)}, u32[]{:S(2)}, u32[]{:S(2)}) %collective-permute-start.14) | collective-permute-done | bytes 655392 | tf_op jit(solution)/shard_map/ppermute | solution.py:43
  88.8 6.3 %collective-permute-start.26 = (bf16[512,256]{1,0:T(8,128)(2,1)}, bf16[512,256]{1,0:T(8,128)(2,1)}, u32[]{:S(2)}, u32[]{:S(2)}) collective-permute-start(bf16[512,256]{1,0:T(8,128)(2,1)} %attend.4.refs_4_), channel_id=1, source_target_pairs={{0,2},{2,4},{4,6},{6,0},{1,3},{3,5},{5,7},{7,1},{8,10},{10,12},{12... | collective-permute-start | bytes 786440 | tf_op jit(solution)/shard_map/ppermute | solution.py:405
  95.1 11.7 %attend.5.refs_0_ = bf16[512,256]{1,0:T(8,128)(2,1)} custom-call(s32[16]{0:T(128)} %slots.9, bf16[16,256,2048]{2,1,0:T(8,128)(2,1)} %bank.9, bf16[1024,2048]{1,0:T(8,128)(2,1)} %get-tuple-element.27.normed, bf16[256,2048]{1,0:T(8,128)(2,1)} %collective-permute-done.9.rest_0_, bf16[2,6,128,128]{3,2,1,0:T(8,128)(2,1)} %copy-done.6, ...), custom_call_target="tpu_custom_call" | custom-call | flops 4831838208 | bytes 8388608 | tf_op jit(solution)/shard_map/attend/pallas_call | solution.py:257
  108.8 2.7 %collective-permute-start.24 = (bf16[512,256]{1,0:T(8,128)(2,1)}, bf16[512,256]{1,0:T(8,128)(2,1)S(1)}, u32[]{:S(2)}, u32[]{:S(2)}) collective-permute-start(bf16[512,256]{1,0:T(8,128)(2,1)} %attend.5.refs_0_), channel_id=1, source_target_pairs={{0,6},{2,0},{4,2},{6,4},{1,7},{3,1},{5,3},{7,5},{8,14},{10,8},{12,... | collective-permute-start | bytes 786440 | tf_op jit(solution)/shard_map/ppermute | solution.py:405
  111.4 11.7 %attend.6.refs_8_ = bf16[512,256]{1,0:T(8,128)(2,1)} custom-call(s32[16]{0:T(128)} %slots.9, bf16[16,256,2048]{2,1,0:T(8,128)(2,1)} %bank.9, bf16[1024,2048]{1,0:T(8,128)(2,1)} %get-tuple-element.27.normed, bf16[256,2048]{1,0:T(8,128)(2,1)} %collective-permute-done.9.rest_0_, bf16[2,10,128,128]{3,2,1,0:T(8,128)(2,1)} %copy-done, ...), custom_call_target="tpu_custom_call" | custom-call | flops 4831838208 | bytes 8388608 | tf_op jit(solution)/shard_map/attend/pallas_call | solution.py:257
  127.7 10.9 %attend.7.refs_0_ = bf16[512,256]{1,0:T(8,128)(2,1)} custom-call(s32[16]{0:T(128)} %slots.9, bf16[16,256,2048]{2,1,0:T(8,128)(2,1)} %bank.9, bf16[1024,2048]{1,0:T(8,128)(2,1)} %get-tuple-element.27.normed, bf16[2,10,128,128]{3,2,1,0:T(8,128)(2,1)} %copy-done, bf16[2,10,128,128]{3,2,1,0:T(8,128)(2,1)} %copy-done.1, bf16[2,10,128,128]{3,2,1,0:T(8,128)(2,1)} %copy-done.2, ...), custom_call_target="tpu_custom_call" | custom-call | flops 4831838208 | bytes 8388608 | tf_op jit(solution)/shard_map/attend/pallas_call | solution.py:257
  138.8 2.6 %collective-permute-start.21 = (bf16[512,256]{1,0:T(8,128)(2,1)}, bf16[512,256]{1,0:T(8,128)(2,1)S(1)}, u32[]{:S(2)}, u32[]{:S(2)}) collective-permute-start(bf16[512,256]{1,0:T(8,128)(2,1)} %attend.7.refs_0_), channel_id=1, source_target_pairs={{0,6},{2,0},{4,2},{6,4},{1,7},{3,1},{5,3},{7,5},{8,14},{10,8},{12,... | collective-permute-start | bytes 786440 | tf_op jit(solution)/shard_map/ppermute | solution.py:405
  145.0 5.2 %project_first.1 = (bf16[1024,512]{1,0:T(8,128)(2,1)}, f32[512,512]{1,0:T(8,128)}, bf16[1024,512]{1,0:T(8,128)(2,1)}) custom-call(bf16[512,256]{1,0:T(8,128)(2,1)} %attend.5.refs_0_, bf16[512,256]{1,0:T(8,128)(2,1)} %copy-done.18, bf16[512,256]{1,0:T(8,128)(2,1)} %copy-done.19, bf16[512,256]{1,0:T(8,128)(2,1)} %copy-done.20, ...), custom_call_target="tpu_custom_call" | custom-call | flops 1073741824 | bytes 8388608 | tf_op jit(solution)/shard_map/project_first/pallas_call | solution.py:325
  150.3 5.3 %collective-permute-done.22.refs_3_ = bf16[512,256]{1,0:T(8,128)(2,1)S(1)} collective-permute-done((bf16[512,256]{1,0:T(8,128)(2,1)}, bf16[512,256]{1,0:T(8,128)(2,1)S(1)}, u32[]{:S(2)}, u32[]{:S(2)}) %collective-permute-start.22) | collective-permute-done | bytes 262176 | tf_op jit(solution)/shard_map/ppermute | solution.py:405
  156.3 3.3 %project_last.1 = bf16[1024,512]{1,0:T(8,128)(2,1)} custom-call(bf16[512,256]{1,0:T(8,128)(2,1)} %attend.7.refs_0_, bf16[512,256]{1,0:T(8,128)(2,1)} %copy-done.23, bf16[512,256]{1,0:T(8,128)(2,1)} %copy-done.25, bf16[512,256]{1,0:T(8,128)(2,1)} %copy-done.26, bf16[1024,512]{1,0:T(8,128)(2,1)} %get-tuple-element.28.refs_4_, ...), custom_call_target="tpu_custom_call", output_to_operand_aliasing={{}: (6, {})} | custom-call | flops 536870912 | bytes 4194304 | tf_op jit(solution)/shard_map/project_last/pallas_call | solution.py:368
  (109 shorter events, 30.2 us)
Async XLA Ops:
  18.7 21.4 %collective-permute-start.5 = (bf16[2,6,128,128]{3,2,1,0:T(8,128)(2,1)S(1)}, bf16[2,6,128,128]{3,2,1,0:T(8,128)(2,1)S(1)}, u32[]{:S(2)}, u32[]{:S(2)}) collective-permute-start(bf16[2,6,128,128]{3,2,1,0:T(8,128)(2,1)S(1)} %pad_maximum_fusion.2.rest_0_.rest_1_), channel_id=1, source_target_pairs={{0,8},{8,0},{16,24},{24,16},{32,40},{40,32},{48,56},{56,48},{64,72... | collective-permute-start | bytes 1179656 | tf_op jit(solution)/shard_map/ppermute | solution.py:43
  20.5 22.9 %collective-permute-start.6 = (bf16[2,6,128,128]{3,2,1,0:T(8,128)(2,1)S(1)}, bf16[2,6,128,128]{3,2,1,0:T(8,128)(2,1)S(1)}, u32[]{:S(2)}, u32[]{:S(2)}) collective-permute-start(bf16[2,6,128,128]{3,2,1,0:T(8,128)(2,1)S(1)} %pad_maximum_fusion.3.rest_1_.rest_2_), channel_id=1, source_target_pairs={{0,8},{8,0},{16,24},{24,16},{32,40},{40,32},{48,56},{56,48},{64,72... | collective-permute-start | bytes 1179656 | tf_op jit(solution)/shard_map/ppermute | solution.py:43
  22.7 25.3 %collective-permute-start.7 = (bf16[2,6,128,128]{3,2,1,0:T(8,128)(2,1)S(1)}, bf16[2,6,128,128]{3,2,1,0:T(8,128)(2,1)S(1)}, u32[]{:S(2)}, u32[]{:S(2)}) collective-permute-start(bf16[2,6,128,128]{3,2,1,0:T(8,128)(2,1)S(1)} %collective-permute-done.3.rest_2_.rest_3_), channel_id=1, source_target_pairs={{0,8},{8,0},{16,24},{24,16},{32,40},{40,32},{48,56},{56,48},{64,72... | collective-permute-start | bytes 1179656 | tf_op jit(solution)/shard_map/ppermute | solution.py:43
  25.7 22.5 %collective-permute-start.8 = (bf16[2,6,128,128]{3,2,1,0:T(8,128)(2,1)S(1)}, bf16[2,6,128,128]{3,2,1,0:T(8,128)(2,1)S(1)}, u32[]{:S(2)}, u32[]{:S(2)}) collective-permute-start(bf16[2,6,128,128]{3,2,1,0:T(8,128)(2,1)S(1)} %collective-permute-done.4.rest_3_.rest_4_), channel_id=1, source_target_pairs={{0,8},{8,0},{16,24},{24,16},{32,40},{40,32},{48,56},{56,48},{64,72... | collective-permute-start | bytes 1179656 | tf_op jit(solution)/shard_map/ppermute | solution.py:43
  35.0 53.8 %collective-permute-start.9 = (bf16[256,2048]{1,0:T(8,128)(2,1)}, bf16[256,2048]{1,0:T(8,128)(2,1)}, u32[]{:S(2)}, u32[]{:S(2)}) collective-permute-start(bf16[256,2048]{1,0:T(8,128)(2,1)} %get-tuple-element.20), channel_id=1, source_target_pairs={{0,8},{8,16},{16,24},{24,32},{32,40},{40,48},{48,56},{56,64},{64,7... | collective-permute-start | bytes 3145736 | tf_op jit(solution)/shard_map/ppermute | solution.py:402
  40.1 20.9 %collective-permute-start.11 = (bf16[10,128,128]{2,1,0:T(8,128)(2,1)}, bf16[10,128,128]{2,1,0:T(8,128)(2,1)S(1)}, u32[]{:S(2)}, u32[]{:S(2)}) collective-permute-start(bf16[10,128,128]{2,1,0:T(8,128)(2,1)} %pack.3), channel_id=1, source_target_pairs={{0,16},{8,24},{16,32},{24,40},{32,48},{40,56},{48,0},{56,8},{64,80... | collective-permute-start | bytes 983048 | tf_op jit(solution)/shard_map/ppermute | solution.py:43
  43.4 27.4 %collective-permute-start.13 = (bf16[10,128,128]{2,1,0:T(8,128)(2,1)}, bf16[10,128,128]{2,1,0:T(8,128)(2,1)S(1)}, u32[]{:S(2)}, u32[]{:S(2)}) collective-permute-start(bf16[10,128,128]{2,1,0:T(8,128)(2,1)} %pack.3), channel_id=1, source_target_pairs={{0,32},{8,40},{16,48},{24,56},{32,0},{40,8},{48,16},{56,24},{64,96... | collective-permute-start | bytes 983048 | tf_op jit(solution)/shard_map/ppermute | solution.py:43
  48.0 22.7 %collective-permute-start.12 = (bf16[10,128,128]{2,1,0:T(8,128)(2,1)}, bf16[10,128,128]{2,1,0:T(8,128)(2,1)}, u32[]{:S(2)}, u32[]{:S(2)}) collective-permute-start(bf16[10,128,128]{2,1,0:T(8,128)(2,1)} %pack.3), channel_id=1, source_target_pairs={{0,48},{8,56},{16,0},{24,8},{32,16},{40,24},{48,32},{56,40},{64,11... | collective-permute-start | bytes 983048 | tf_op jit(solution)/shard_map/ppermute | solution.py:43
  70.8 16.9 %collective-permute-start.14 = (bf16[2,10,128,128]{3,2,1,0:T(8,128)(2,1)S(1)}, bf16[2,10,128,128]{3,2,1,0:T(8,128)(2,1)S(1)}, u32[]{:S(2)}, u32[]{:S(2)}) collective-permute-start(bf16[2,10,128,128]{3,2,1,0:T(8,128)(2,1)S(1)} %pad_maximum_fusion.rest_1_.rest_0_.refs_12_), channel_id=1, source_target_pairs={{0,64},{8,72},{16,80},{24,88},{32,96},{40,104},{48,112},{56,120},{... | collective-permute-start | bytes 1966088 | tf_op jit(solution)/shard_map/ppermute | solution.py:43
  76.4 12.4 %collective-permute-start.15 = (bf16[2,10,128,128]{3,2,1,0:T(8,128)(2,1)S(1)}, bf16[2,10,128,128]{3,2,1,0:T(8,128)(2,1)S(1)}, u32[]{:S(2)}, u32[]{:S(2)}) collective-permute-start(bf16[2,10,128,128]{3,2,1,0:T(8,128)(2,1)S(1)} %pad_maximum_fusion.1.rest_2_.rest_1_.refs_13_), channel_id=1, source_target_pairs={{0,65},{8,73},{16,81},{24,89},{32,97},{40,105},{48,113},{56,121},{... | collective-permute-start | bytes 1966088 | tf_op jit(solution)/shard_map/ppermute | solution.py:43
  78.9 27.9 %collective-permute-start.16 = (bf16[2,10,128,128]{3,2,1,0:T(8,128)(2,1)S(1)}, bf16[2,10,128,128]{3,2,1,0:T(8,128)(2,1)S(1)}, u32[]{:S(2)}, u32[]{:S(2)}) collective-permute-start(bf16[2,10,128,128]{3,2,1,0:T(8,128)(2,1)S(1)} %pad_maximum_fusion.rest_1_.rest_0_.refs_12_), channel_id=1, source_target_pairs={{0,8},{8,0},{16,24},{24,16},{32,40},{40,32},{48,56},{56,48},{64,72... | collective-permute-start | bytes 1966088 | tf_op jit(solution)/shard_map/ppermute | solution.py:43
  78.9 28.0 %collective-permute-start.17 = (bf16[2,10,128,128]{3,2,1,0:T(8,128)(2,1)S(1)}, bf16[2,10,128,128]{3,2,1,0:T(8,128)(2,1)S(1)}, u32[]{:S(2)}, u32[]{:S(2)}) collective-permute-start(bf16[2,10,128,128]{3,2,1,0:T(8,128)(2,1)S(1)} %pad_maximum_fusion.1.rest_2_.rest_1_.refs_13_), channel_id=1, source_target_pairs={{0,8},{8,0},{16,24},{24,16},{32,40},{40,32},{48,56},{56,48},{64,72... | collective-permute-start | bytes 1966088 | tf_op jit(solution)/shard_map/ppermute | solution.py:43
  87.7 21.1 %collective-permute-start.18 = (bf16[2,10,128,128]{3,2,1,0:T(8,128)(2,1)S(1)}, bf16[2,10,128,128]{3,2,1,0:T(8,128)(2,1)}, u32[]{:S(2)}, u32[]{:S(2)}) collective-permute-start(bf16[2,10,128,128]{3,2,1,0:T(8,128)(2,1)S(1)} %collective-permute-done.14.rest_3_.rest_2_.refs_14_), channel_id=1, source_target_pairs={{0,8},{8,0},{16,24},{24,16},{32,40},{40,32},{48,56},{56,48},{64,72... | collective-permute-start | bytes 1966088 | tf_op jit(solution)/shard_map/ppermute | solution.py:43
  88.8 20.0 %collective-permute-start.19 = (bf16[2,10,128,128]{3,2,1,0:T(8,128)(2,1)S(1)}, bf16[2,10,128,128]{3,2,1,0:T(8,128)(2,1)}, u32[]{:S(2)}, u32[]{:S(2)}) collective-permute-start(bf16[2,10,128,128]{3,2,1,0:T(8,128)(2,1)S(1)} %collective-permute-done.15.rest_4_.rest_3_.refs_15_), channel_id=1, source_target_pairs={{0,8},{8,0},{16,24},{24,16},{32,40},{40,32},{48,56},{56,48},{64,72... | collective-permute-start | bytes 1966088 | tf_op jit(solution)/shard_map/ppermute | solution.py:43
  88.8 34.4 %collective-permute-start.26 = (bf16[512,256]{1,0:T(8,128)(2,1)}, bf16[512,256]{1,0:T(8,128)(2,1)}, u32[]{:S(2)}, u32[]{:S(2)}) collective-permute-start(bf16[512,256]{1,0:T(8,128)(2,1)} %attend.4.refs_4_), channel_id=1, source_target_pairs={{0,2},{2,4},{4,6},{6,0},{1,3},{3,5},{5,7},{7,1},{8,10},{10,12},{12... | collective-permute-start | bytes 786440 | tf_op jit(solution)/shard_map/ppermute | solution.py:405
  106.9 17.0 %collective-permute-start.27 = (bf16[512,256]{1,0:T(8,128)(2,1)}, bf16[512,256]{1,0:T(8,128)(2,1)S(1)}, u32[]{:S(2)}, u32[]{:S(2)}) collective-permute-start(bf16[512,256]{1,0:T(8,128)(2,1)} %attend.4.refs_4_), channel_id=1, source_target_pairs={{0,6},{2,0},{4,2},{6,4},{1,7},{3,1},{5,3},{7,5},{8,14},{10,8},{12,... | collective-permute-start | bytes 786440 | tf_op jit(solution)/shard_map/ppermute | solution.py:405
  107.0 17.7 %collective-permute-start.28 = (bf16[512,256]{1,0:T(8,128)(2,1)}, bf16[512,256]{1,0:T(8,128)(2,1)S(1)}, u32[]{:S(2)}, u32[]{:S(2)}) collective-permute-start(bf16[512,256]{1,0:T(8,128)(2,1)} %attend.4.refs_4_), channel_id=1, source_target_pairs={{0,4},{2,6},{4,0},{6,2},{1,5},{3,7},{5,1},{7,3},{8,12},{10,14},{12... | collective-permute-start | bytes 786440 | tf_op jit(solution)/shard_map/ppermute | solution.py:405
  108.7 17.8 %collective-permute-start.23 = (bf16[512,256]{1,0:T(8,128)(2,1)}, bf16[512,256]{1,0:T(8,128)(2,1)S(1)}, u32[]{:S(2)}, u32[]{:S(2)}) collective-permute-start(bf16[512,256]{1,0:T(8,128)(2,1)} %attend.5.refs_0_), channel_id=1, source_target_pairs={{0,2},{2,4},{4,6},{6,0},{1,3},{3,5},{5,7},{7,1},{8,10},{10,12},{12... | collective-permute-start | bytes 786440 | tf_op jit(solution)/shard_map/ppermute | solution.py:405
  108.8 29.9 %collective-permute-start.24 = (bf16[512,256]{1,0:T(8,128)(2,1)}, bf16[512,256]{1,0:T(8,128)(2,1)S(1)}, u32[]{:S(2)}, u32[]{:S(2)}) collective-permute-start(bf16[512,256]{1,0:T(8,128)(2,1)} %attend.5.refs_0_), channel_id=1, source_target_pairs={{0,6},{2,0},{4,2},{6,4},{1,7},{3,1},{5,3},{7,5},{8,14},{10,8},{12,... | collective-permute-start | bytes 786440 | tf_op jit(solution)/shard_map/ppermute | solution.py:405
  123.2 15.6 %collective-permute-start.25 = (bf16[512,256]{1,0:T(8,128)(2,1)S(1)}, bf16[512,256]{1,0:T(8,128)(2,1)S(1)}, u32[]{:S(2)}, u32[]{:S(2)}) collective-permute-start(bf16[512,256]{1,0:T(8,128)(2,1)S(1)} %copy-done.15), channel_id=1, source_target_pairs={{0,4},{2,6},{4,0},{6,2},{1,5},{3,7},{5,1},{7,3},{8,12},{10,14},{12... | collective-permute-start | bytes 786440 | tf_op jit(solution)/shard_map/ppermute | solution.py:405
  123.9 17.5 %collective-permute-start.29 = (bf16[512,256]{1,0:T(8,128)(2,1)}, bf16[512,256]{1,0:T(8,128)(2,1)S(1)}, u32[]{:S(2)}, u32[]{:S(2)}) collective-permute-start(bf16[512,256]{1,0:T(8,128)(2,1)} %attend.6.refs_8_), channel_id=1, source_target_pairs={{0,2},{2,4},{4,6},{6,0},{1,3},{3,5},{5,7},{7,1},{8,10},{10,12},{12... | collective-permute-start | bytes 786440 | tf_op jit(solution)/shard_map/ppermute | solution.py:405
  124.7 17.3 %collective-permute-start.30 = (bf16[512,256]{1,0:T(8,128)(2,1)}, bf16[512,256]{1,0:T(8,128)(2,1)S(1)}, u32[]{:S(2)}, u32[]{:S(2)}) collective-permute-start(bf16[512,256]{1,0:T(8,128)(2,1)} %attend.6.refs_8_), channel_id=1, source_target_pairs={{0,6},{2,0},{4,2},{6,4},{1,7},{3,1},{5,3},{7,5},{8,14},{10,8},{12,... | collective-permute-start | bytes 786440 | tf_op jit(solution)/shard_map/ppermute | solution.py:405
  126.6 17.7 %collective-permute-start.31 = (bf16[512,256]{1,0:T(8,128)(2,1)}, bf16[512,256]{1,0:T(8,128)(2,1)S(1)}, u32[]{:S(2)}, u32[]{:S(2)}) collective-permute-start(bf16[512,256]{1,0:T(8,128)(2,1)} %attend.6.refs_8_), channel_id=1, source_target_pairs={{0,4},{2,6},{4,0},{6,2},{1,5},{3,7},{5,1},{7,3},{8,12},{10,14},{12... | collective-permute-start | bytes 786440 | tf_op jit(solution)/shard_map/ppermute | solution.py:405
  141.4 14.1 %collective-permute-start.22 = (bf16[512,256]{1,0:T(8,128)(2,1)}, bf16[512,256]{1,0:T(8,128)(2,1)S(1)}, u32[]{:S(2)}, u32[]{:S(2)}) collective-permute-start(bf16[512,256]{1,0:T(8,128)(2,1)} %attend.7.refs_0_), channel_id=1, source_target_pairs={{0,4},{2,6},{4,0},{6,2},{1,5},{3,7},{5,1},{7,3},{8,12},{10,14},{12... | collective-permute-start | bytes 786440 | tf_op jit(solution)/shard_map/ppermute | solution.py:405
  (36 other events, 381.5 us)
